TPU v7x, 512 devices: a whole 4x4x16 slice. The times are simulated.
512 devices in a mesh: harm: 32 (over z, x_hi), slab: 16 (over y, x_lo, core).
Axes of the slice: x: 4 (x_hi: 2, x_lo: 2; x = x_hi * 2 + x_lo), y: 4, z: 16, core: 2. Of those that a mesh axis runs over, the one named last changes fastest.
Arguments:
- harmonics: float32 [32, 2, 5, 32, 2048], P('harm', None, None, 'slab'), may hold values from -4 to 4
- mean_flow: float32 [5, 32, 2048], P(None, 'slab'), may hold values from 0.5 to 13.5
- freq_index: int32 [32], P('harm'), may hold values from 1 to 8
- wall_mask: int32 [32, 2048], P('slab'), may hold values 0 or 1
- jacobian_x: float32 [5, 5], replicated, may hold values from -2.5 to 2.5
- jacobian_y: float32 [5, 5], replicated, may hold values from -2.5 to 2.5
Outputs:
- mean_next: float32 [5, 32, 2048], P(None, 'slab')
- harmonics_next: float32 [32, 2, 5, 32, 2048], P('harm', None, None, 'slab')
All inputs are finite; a program needn't handle non-finite values. No bound on the sum of `wall_mask` on one device may be relied on, other than what follows from the above.
Results may differ from a plain program's by a relative error of at most 0.00018.
Values sent between devices are 32-bit elements; how exact they have to be, the bound alone decides.
No kernel may reach another device: no remote copies, remote signals or barrier semaphores. Data moves between devices by JAX's collectives and lax.ppermute only.
A program may use at most 64 MiB of HBM per device.

v0:
```python
import jax
import jax.numpy as jnp
from jax import lax
from jax.sharding import PartitionSpec as P

NZ = 64


EPS_FOURTH = 0.05
COURANT = 0.9
OMEGA_BASE = 0.25
WALL_RATE = 2.0
HUB_RADIUS = 0.5
SECTION_RATES = (0.25, 1.0 / 3.0, 0.5, 1.0)
STRESS_PAIRS = ((1, 1), (1, 2), (1, 3), (2, 2), (2, 3), (3, 3), (4, 1), (4, 2), (4, 3))


def from_everyone(shard, axis):
    count = lax.axis_size(axis)
    return lax.all_to_all(
        jnp.broadcast_to(shard[None], (count, *shard.shape)), axis, 0, 0, tiled=True
    )


def taken_together(shard, axis):
    everything = from_everyone(shard, axis)
    return jnp.sum(everything, axis=0)


def with_halo(cells, sides, width):
    for axis, dim in sides:
        count = lax.axis_size(axis)
        ends = count - 1
        head = lax.slice_in_dim(cells, 0, width, axis=dim)
        tail = lax.slice_in_dim(cells, cells.shape[dim] - width, cells.shape[dim], axis=dim)
        cells = jnp.concatenate(
            [
                lax.ppermute(tail, axis, [(i, (i + 1) % count) for i in range(ends)]),
                cells,
                lax.ppermute(head, axis, [((i + 1) % count, i) for i in range(ends)]),
            ],
            axis=dim,
        )
    return cells


def split_up(shard, dim, count):
    dims = shard.shape
    parts = shard.reshape(*dims[:dim], count, dims[dim] // count, *dims[dim + 1 :])
    return jnp.moveaxis(parts, dim, 0)


def sum_at_owner(shard, axis, dim):
    parts = split_up(shard, dim, lax.axis_size(axis))
    arrived = lax.all_to_all(parts, axis, split_axis=0, concat_axis=0, tiled=True)
    return arrived.sum(axis=0)


def rows_for(lines, count):
    spare = -lines.shape[0] % count
    if not spare:
        return lines
    return jnp.concatenate([lines, jnp.zeros((spare, *lines.shape[1:]), lines.dtype)])


def in_order(parts, dim):
    parts = jnp.moveaxis(parts, 0, dim)
    dims = parts.shape
    return parts.reshape(*dims[:dim], dims[dim] * dims[dim + 1], *dims[dim + 2 :])


def collect(shard, axis, dim):
    parts = from_everyone(shard, axis)
    return in_order(parts, dim)


def nested_sum(shard, axes):
    lines = shard.reshape(-1)
    own = sum_at_owner(rows_for(lines, lax.axis_size(axes)), axes, 0)
    whole = collect(own, axes, 0)
    return whole[: len(lines)].reshape(shard.shape)


def apply_matrix(matrix, values):
    return jnp.einsum("ab,...bxp->...axp", matrix, values, precision=lax.Precision.HIGHEST)


def diff_across(values):
    return (jnp.roll(values, -NZ, axis=-1) - jnp.roll(values, NZ, axis=-1)) * 0.5


def fourth_across(values):
    return (
        jnp.roll(values, -2 * NZ, axis=-1)
        - 4.0 * jnp.roll(values, -NZ, axis=-1)
        + 6.0 * values
        - 4.0 * jnp.roll(values, NZ, axis=-1)
        + jnp.roll(values, 2 * NZ, axis=-1)
    )


def diff_along(padded):
    return (padded[..., 3:-1, :] - padded[..., 1:-3, :]) * 0.5


def fourth_along(padded):
    return (
        padded[..., 4:, :]
        - 4.0 * padded[..., 3:-1, :]
        + 6.0 * padded[..., 2:-2, :]
        - 4.0 * padded[..., 1:-3, :]
        + padded[..., :-4, :]
    )


def harmonic_residual(harm_pad, momentum_pad, omegas, wall_cells, jac_x, jac_y):
    center = harm_pad[..., 2:-2, :]
    flux_x = apply_matrix(jac_x, harm_pad * momentum_pad)
    flux_y = apply_matrix(jac_y, center)
    rotation = jnp.stack([center[..., 1, :, :, :], -center[..., 0, :, :, :]], axis=-4) * omegas
    return (
        rotation
        - diff_along(flux_x)
        - diff_across(flux_y)
        - EPS_FOURTH * (fourth_along(harm_pad) + fourth_across(center))
        - WALL_RATE * wall_cells * center
    )


def stresses(values):
    fields = []
    for first, second in STRESS_PAIRS:
        product = values[..., first, :, :] * values[..., second, :, :]
        fields.append(0.5 * jnp.sum(product, axis=tuple(range(product.ndim - 2))))
    return jnp.stack(fields, axis=0)


def forcing(stress_pad, radius):
    center = stress_pad[:, 1:-1, :]
    grad_x = (stress_pad[:, 2:, :] - stress_pad[:, :-2, :]) * 0.5
    grad_y = diff_across(center)
    first = -grad_x[0] - grad_y[1]
    second = -grad_x[1] - grad_y[3] - 2.0 * center[4] / radius
    third = -grad_x[2] - grad_y[4] + (center[3] - center[5]) / radius
    fourth = -grad_x[6] - grad_y[7] - center[8] / radius
    return jnp.stack([first, second, third, fourth], axis=0)


def mean_residual(mean_pad, forcing_terms, jac_x, jac_y):
    center = mean_pad[:, 2:-2, :]
    residual = (
        -diff_along(apply_matrix(jac_x, mean_pad))
        - diff_across(apply_matrix(jac_y, center))
        - EPS_FOURTH * (fourth_along(mean_pad) + fourth_across(center))
    )
    zeros_row = jnp.zeros_like(forcing_terms[:1])
    return residual + jnp.concatenate([zeros_row, forcing_terms], axis=0)


def shards(harmonics, mean_flow, freq_index, wall_mask, jacobian_x, jacobian_y):
    owned = harmonics.shape[0]
    slab_cells = mean_flow.shape[1]
    plane_count = mean_flow.shape[2]
    radius = HUB_RADIUS + ((jnp.arange(plane_count) % NZ).astype(jnp.float32) + 0.5) / NZ
    wall_cells = wall_mask.astype(jnp.float32)
    omegas = (OMEGA_BASE * freq_index.astype(jnp.float32)).reshape(owned, 1, 1, 1, 1)
    speed_total = taken_together(jnp.sum(mean_flow[1] * mean_flow[1]), "slab")
    cell_count = slab_cells * lax.axis_size("slab") * plane_count
    time_step = COURANT / (1.0 + jnp.sqrt(speed_total / cell_count))
    harm_now, mean_now = (harmonics, mean_flow)
    for section_rate in SECTION_RATES:
        stacked = jnp.concatenate(
            [harm_now.reshape(owned * 2, 5, slab_cells, plane_count), mean_now[None]], axis=0
        )
        padded = with_halo(stacked, (("slab", 2),), 2)
        harm_pad = padded[: 2 * owned].reshape(owned, 2, 5, slab_cells + 4, plane_count)
        mean_pad = padded[2 * owned]
        harm_res = harmonic_residual(
            harm_pad, mean_pad[1], omegas, wall_cells, jacobian_x, jacobian_y
        )
        partial_terms = forcing(stresses(harm_pad[..., 1:-1, :]), radius)
        forcing_terms = nested_sum(partial_terms, "harm")
        mean_res = mean_residual(mean_pad, forcing_terms, jacobian_x, jacobian_y)
        harm_now = harmonics + section_rate * time_step * harm_res
        mean_now = mean_flow + section_rate * time_step * mean_res
    return (mean_now, harm_now)


def solution(mesh):
    placed = (
        P("harm", None, None, "slab", None),
        P(None, "slab", None),
        P("harm"),
        P("slab", None),
        P(),
        P(),
    )
    return jax.shard_map(
        shards,
        mesh=mesh,
        in_specs=placed,
        out_specs=(P(None, "slab", None), P("harm", None, None, "slab", None)),
        check_vma=False,
    )
```

profile of v0, /device:TPU:16, one launch (start us, length us, event | category | flops | bytes accessed | tf_op | source)
XLA Modules:
  0.0 283.8 jit_solution(8491351300656256550)
XLA Ops:
  0.7 1.0 copy.119
  1.6 1.0 copy.118
  2.7 2.7 collective-permute-start.1
  5.4 1.9 collective-permute-start
  7.3 1.3 multiply_reduce_fusion.36
  8.7 1.2 broadcast_in_dim.18
  9.9 8.7 %all-to-all-start = ((f32[16,1,1]{2,1,0:T(1,128)}), f32[16,1,1]{2,1,0:T(1,128)S(1)}, u32[]{:S(2)}, u32[]{:S(2)}) async-start(f32[16,1,1]{2,1,0:T(1,128)} %broadcast_in_dim.18), calls=%async_computation | async-start | bytes 16384 | tf_op jit(solution)/shard_map/all_to_all | solution.py:20
  19.9 2.5 all-to-all-done
  25.3 1.1 multiply_reduce_fusion.28
  28.9 1.1 fusion.195
  33.1 16.1 %all-to-all-start.1 = ((f32[32,1,512]{2,1,0:T(1,128)}), f32[32,1,512]{2,1,0:T(1,128)}, u32[]{:S(2)}, u32[]{:S(2)}) async-start(f32[32,1,512]{2,1,0:T(1,128)} %all_to_all.45), calls=%async_computation.1 | async-start | bytes 131072 | tf_op jit(solution)/shard_map/all_to_all | solution.py:55
  50.1 1.9 fusion.14
  52.1 12.3 %all-to-all-done.1 = f32[32,1,512]{2,1,0:T(1,128)} async-done(((f32[32,1,512]{2,1,0:T(1,128)}), f32[32,1,512]{2,1,0:T(1,128)}, u32[]{:S(2)}, u32[]{:S(2)}) %all-to-all-start.1) | async-done | bytes 65568 | tf_op jit(solution)/shard_map/all_to_all | solution.py:55
  64.4 0.9 reduce_sum.389
  65.9 3.9 %all-to-all-start.2 = ((f32[32,1,512]{2,1,0:T(1,128)}), f32[32,1,512]{2,1,0:T(1,128)S(1)}, u32[]{:S(2)}, u32[]{:S(2)}) async-start(f32[32,1,512]{2,1,0:T(1,128)} %broadcast_in_dim.20), calls=%async_computation.2 | async-start | bytes 131072 | tf_op jit(solution)/shard_map/all_to_all | solution.py:20
  70.3 14.7 %all-to-all-done.2 = f32[32,1,512]{2,1,0:T(1,128)S(1)} async-done(((f32[32,1,512]{2,1,0:T(1,128)}), f32[32,1,512]{2,1,0:T(1,128)S(1)}, u32[]{:S(2)}, u32[]{:S(2)}) %all-to-all-start.2) | async-done | bytes 65568 | tf_op jit(solution)/shard_map/all_to_all | solution.py:20
  85.6 1.9 collective-permute-start.3
  87.5 2.6 collective-permute-start.2
  90.1 5.2 %collective-permute-done.3 = f32[3,5,2,2048]{3,1,2,0:T(8,128)S(1)} collective-permute-done((f32[3,5,2,2048]{3,1,2,0:T(8,128)S(1)}, f32[3,5,2,2048]{3,1,2,0:T(8,128)S(1)}, u32[]{:S(2)}, u32[]{:S(2)}) %collective-permute-start.3) | collective-permute-done | bytes 245792 | tf_op jit(solution)/shard_map/ppermute | solution.py:40
  95.2 3.1 %collective-permute-done.2 = f32[3,5,2,2048]{3,1,2,0:T(8,128)S(1)} collective-permute-done((f32[3,5,2,2048]{3,1,2,0:T(8,128)S(1)}, f32[3,5,2,2048]{3,1,2,0:T(8,128)S(1)}, u32[]{:S(2)}, u32[]{:S(2)}) %collective-permute-start.2) | collective-permute-done | bytes 245792 | tf_op jit(solution)/shard_map/ppermute | solution.py:38
  103.4 1.1 multiply_reduce_fusion.19
  109.6 4.6 %all-to-all-start.3 = ((f32[32,1,512]{2,1,0:T(1,128)}), f32[32,1,512]{2,1,0:T(1,128)}, u32[]{:S(2)}, u32[]{:S(2)}) async-start(f32[32,1,512]{2,1,0:T(1,128)} %all_to_all.48), calls=%async_computation.3 | async-start | bytes 131072 | tf_op jit(solution)/shard_map/all_to_all | solution.py:55
  114.2 1.8 fusion.13
  116.1 13.3 %all-to-all-done.3 = f32[32,1,512]{2,1,0:T(1,128)} async-done(((f32[32,1,512]{2,1,0:T(1,128)}), f32[32,1,512]{2,1,0:T(1,128)}, u32[]{:S(2)}, u32[]{:S(2)}) %all-to-all-start.3) | async-done | bytes 65568 | tf_op jit(solution)/shard_map/all_to_all | solution.py:55
  131.0 3.9 %all-to-all-start.4 = ((f32[32,1,512]{2,1,0:T(1,128)}), f32[32,1,512]{2,1,0:T(1,128)S(1)}, u32[]{:S(2)}, u32[]{:S(2)}) async-start(f32[32,1,512]{2,1,0:T(1,128)} %broadcast_in_dim.22), calls=%async_computation.4 | async-start | bytes 131072 | tf_op jit(solution)/shard_map/all_to_all | solution.py:20
  135.4 14.7 %all-to-all-done.4 = f32[32,1,512]{2,1,0:T(1,128)S(1)} async-done(((f32[32,1,512]{2,1,0:T(1,128)}), f32[32,1,512]{2,1,0:T(1,128)S(1)}, u32[]{:S(2)}, u32[]{:S(2)}) %all-to-all-start.4) | async-done | bytes 65568 | tf_op jit(solution)/shard_map/all_to_all | solution.py:20
  150.7 1.9 collective-permute-start.5
  152.6 2.4 collective-permute-start.4
  155.0 4.5 %collective-permute-done.5 = f32[3,5,2,2048]{3,1,2,0:T(8,128)S(1)} collective-permute-done((f32[3,5,2,2048]{3,1,2,0:T(8,128)S(1)}, f32[3,5,2,2048]{3,1,2,0:T(8,128)S(1)}, u32[]{:S(2)}, u32[]{:S(2)}) %collective-permute-start.5) | collective-permute-done | bytes 245792 | tf_op jit(solution)/shard_map/ppermute | solution.py:40
  159.5 5.0 %collective-permute-done.4 = f32[3,5,2,2048]{3,1,2,0:T(8,128)S(1)} collective-permute-done((f32[3,5,2,2048]{3,1,2,0:T(8,128)S(1)}, f32[3,5,2,2048]{3,1,2,0:T(8,128)S(1)}, u32[]{:S(2)}, u32[]{:S(2)}) %collective-permute-start.4) | collective-permute-done | bytes 245792 | tf_op jit(solution)/shard_map/ppermute | solution.py:38
  169.7 1.1 multiply_reduce_fusion.10
  175.9 4.8 %all-to-all-start.5 = ((f32[32,1,512]{2,1,0:T(1,128)}), f32[32,1,512]{2,1,0:T(1,128)}, u32[]{:S(2)}, u32[]{:S(2)}) async-start(f32[32,1,512]{2,1,0:T(1,128)} %all_to_all.51), calls=%async_computation.5 | async-start | bytes 131072 | tf_op jit(solution)/shard_map/all_to_all | solution.py:55
  180.7 1.8 fusion.12
  182.7 13.1 %all-to-all-done.5 = f32[32,1,512]{2,1,0:T(1,128)} async-done(((f32[32,1,512]{2,1,0:T(1,128)}), f32[32,1,512]{2,1,0:T(1,128)}, u32[]{:S(2)}, u32[]{:S(2)}) %all-to-all-start.5) | async-done | bytes 65568 | tf_op jit(solution)/shard_map/all_to_all | solution.py:55
  195.7 0.9 reduce_sum.409
  197.3 3.9 %all-to-all-start.6 = ((f32[32,1,512]{2,1,0:T(1,128)}), f32[32,1,512]{2,1,0:T(1,128)S(1)}, u32[]{:S(2)}, u32[]{:S(2)}) async-start(f32[32,1,512]{2,1,0:T(1,128)} %broadcast_in_dim.24), calls=%async_computation.6 | async-start | bytes 131072 | tf_op jit(solution)/shard_map/all_to_all | solution.py:20
  201.7 14.6 %all-to-all-done.6 = f32[32,1,512]{2,1,0:T(1,128)S(1)} async-done(((f32[32,1,512]{2,1,0:T(1,128)}), f32[32,1,512]{2,1,0:T(1,128)S(1)}, u32[]{:S(2)}, u32[]{:S(2)}) %all-to-all-start.6) | async-done | bytes 65568 | tf_op jit(solution)/shard_map/all_to_all | solution.py:20
  217.0 1.9 collective-permute-start.7
  218.9 2.4 collective-permute-start.6
  221.3 5.3 %collective-permute-done.7 = f32[3,5,2,2048]{3,1,2,0:T(8,128)S(1)} collective-permute-done((f32[3,5,2,2048]{3,1,2,0:T(8,128)S(1)}, f32[3,5,2,2048]{3,1,2,0:T(8,128)S(1)}, u32[]{:S(2)}, u32[]{:S(2)}) %collective-permute-start.7) | collective-permute-done | bytes 245792 | tf_op jit(solution)/shard_map/ppermute | solution.py:40
  226.6 3.2 %collective-permute-done.6 = f32[3,5,2,2048]{3,1,2,0:T(8,128)S(1)} collective-permute-done((f32[3,5,2,2048]{3,1,2,0:T(8,128)S(1)}, f32[3,5,2,2048]{3,1,2,0:T(8,128)S(1)}, u32[]{:S(2)}, u32[]{:S(2)}) %collective-permute-start.6) | collective-permute-done | bytes 245792 | tf_op jit(solution)/shard_map/ppermute | solution.py:38
  234.9 1.1 multiply_reduce_fusion.1
  239.3 1.7 convolution_bitcast_fusion
  242.1 4.6 %all-to-all-start.7 = ((f32[32,1,512]{2,1,0:T(1,128)}), f32[32,1,512]{2,1,0:T(1,128)}, u32[]{:S(2)}, u32[]{:S(2)}) async-start(f32[32,1,512]{2,1,0:T(1,128)} %all_to_all.54), calls=%async_computation.7 | async-start | bytes 131072 | tf_op jit(solution)/shard_map/all_to_all | solution.py:55
  246.7 2.0 copy_add_fusion
  248.8 13.0 %all-to-all-done.7 = f32[32,1,512]{2,1,0:T(1,128)} async-done(((f32[32,1,512]{2,1,0:T(1,128)}), f32[32,1,512]{2,1,0:T(1,128)}, u32[]{:S(2)}, u32[]{:S(2)}) %all-to-all-start.7) | async-done | bytes 65568 | tf_op jit(solution)/shard_map/all_to_all | solution.py:55
  263.4 3.9 %all-to-all-start.8 = ((f32[32,1,512]{2,1,0:T(1,128)}), f32[32,1,512]{2,1,0:T(1,128)S(1)}, u32[]{:S(2)}, u32[]{:S(2)}) async-start(f32[32,1,512]{2,1,0:T(1,128)} %broadcast_in_dim.26), calls=%async_computation.8 | async-start | bytes 131072 | tf_op jit(solution)/shard_map/all_to_all | solution.py:20
  268.6 14.0 %all-to-all-done.8 = f32[32,1,512]{2,1,0:T(1,128)S(1)} async-done(((f32[32,1,512]{2,1,0:T(1,128)}), f32[32,1,512]{2,1,0:T(1,128)S(1)}, u32[]{:S(2)}, u32[]{:S(2)}) %all-to-all-start.8) | async-done | bytes 65568 | tf_op jit(solution)/shard_map/all_to_all | solution.py:20
  (262 shorter events, 48.9 us)
Async XLA Ops:
  0.6 48.5 %copy-start = (f32[5,5]{1,0:T(8,128)S(1)}, f32[5,5]{1,0:T(8,128)}, u32[]{:S(2)}) copy-start(f32[5,5]{1,0:T(8,128)} %param.10) | copy-start | bytes 304
  0.6 18.0 %copy-start.34 = (s32[2,2048]{1,0:T(2,128)S(1)}, s32[2,2048]{1,0:T(2,128)}, u32[]{:S(2)}) copy-start(s32[2,2048]{1,0:T(2,128)} %param.9) | copy-start | bytes 49156
  2.7 21.1 %collective-permute-start.1 = (f32[3,5,2,2048]{3,1,2,0:T(8,128)S(1)}, f32[3,5,2,2048]{3,1,2,0:T(8,128)S(1)}, u32[]{:S(2)}, u32[]{:S(2)}) collective-permute-start(f32[3,5,2,2048]{3,1,2,0:T(8,128)S(1)} %pad_maximum_fusion.4), channel_id=1, source_target_pairs={{1,0},{2,1},{3,2},{4,3},{5,4},{6,5},{7,6},{8,7},{9,8},{10,9},{11,1... | collective-permute-start | bytes 737288 | tf_op jit(solution)/shard_map/ppermute | solution.py:40
  5.4 18.4 %collective-permute-start = (f32[3,5,2,2048]{3,1,2,0:T(8,128)S(1)}, f32[3,5,2,2048]{3,1,2,0:T(8,128)S(1)}, u32[]{:S(2)}, u32[]{:S(2)}) collective-permute-start(f32[3,5,2,2048]{3,1,2,0:T(8,128)S(1)} %pad_maximum_fusion.4), channel_id=1, source_target_pairs={{0,1},{1,2},{2,3},{3,4},{4,5},{5,6},{6,7},{7,8},{8,9},{9,10},{10,1... | collective-permute-start | bytes 737288 | tf_op jit(solution)/shard_map/ppermute | solution.py:38
  9.9 12.5 %all-to-all-start = ((f32[16,1,1]{2,1,0:T(1,128)}), f32[16,1,1]{2,1,0:T(1,128)S(1)}, u32[]{:S(2)}, u32[]{:S(2)}) async-start(f32[16,1,1]{2,1,0:T(1,128)} %broadcast_in_dim.18), calls=%async_computation | async-start | bytes 16384 | tf_op jit(solution)/shard_map/all_to_all | solution.py:20
  31.0 18.1 %copy-start.32 = (f32[1,1,6,2048]{3,2,1,0:T(8,128)S(1)}, f32[1,1,6,2048]{3,2,1,0:T(8,128)}, u32[]{:S(2)}) copy-start(f32[1,1,6,2048]{3,2,1,0:T(8,128)} %copy.123) | copy-start | bytes 147460
  32.2 17.8 %copy-start.1 = (f32[1,2,5,2,2048]{4,3,2,1,0:T(2,128)S(1)}, f32[1,2,5,2,2048]{4,3,2,1,0:T(2,128)}, u32[]{:S(2)}) copy-start(f32[1,2,5,2,2048]{4,3,2,1,0:T(2,128)} %param.6) | copy-start | bytes 491524
  32.2 17.8 %copy-start.4 = (f32[1,2,5,2,1984]{4,2,3,1,0:T(8,128)S(1)}, f32[1,2,5,2,1984]{4,2,3,1,0:T(8,128)}, u32[]{:S(2)}) copy-start(f32[1,2,5,2,1984]{4,2,3,1,0:T(8,128)} %get-tuple-element.84) | copy-start | bytes 476164
  32.2 17.8 %copy-start.5 = (f32[1,2,5,2,1984]{4,2,3,1,0:T(8,128)S(1)}, f32[1,2,5,2,1984]{4,2,3,1,0:T(8,128)}, u32[]{:S(2)}) copy-start(f32[1,2,5,2,1984]{4,2,3,1,0:T(8,128)} %get-tuple-element.85) | copy-start | bytes 476164
  32.2 17.8 %copy-start.30 = (f32[2,2048]{1,0:T(2,128)S(1)}, f32[2,2048]{1,0:T(2,128)}, u32[]{:S(2)}) copy-start(f32[2,2048]{1,0:T(2,128)} %convert_multiply_fusion) | copy-start | bytes 49156
  32.2 17.8 %copy-start.33 = (f32[1,2,5,2,128]{4,2,3,1,0:T(8,128)S(1)}, f32[1,2,5,2,128]{4,2,3,1,0:T(8,128)}, u32[]{:S(2)}) copy-start(f32[1,2,5,2,128]{4,2,3,1,0:T(8,128)} %get-tuple-element.78) | copy-start | bytes 30724
  33.1 31.3 %all-to-all-start.1 = ((f32[32,1,512]{2,1,0:T(1,128)}), f32[32,1,512]{2,1,0:T(1,128)}, u32[]{:S(2)}, u32[]{:S(2)}) async-start(f32[32,1,512]{2,1,0:T(1,128)} %all_to_all.45), calls=%async_computation.1 | async-start | bytes 131072 | tf_op jit(solution)/shard_map/all_to_all | solution.py:55
  51.9 33.3 %copy-start.2 = (f32[5,2,2048]{2,1,0:T(2,128)S(1)}, f32[5,2,2048]{2,1,0:T(2,128)}, u32[]{:S(2)}) copy-start(f32[5,2,2048]{2,1,0:T(2,128)} %param.7) | copy-start | bytes 245764
  51.9 33.3 %copy-start.20 = (f32[5,2,1984]{2,0,1:T(8,128)S(1)}, f32[5,2,1984]{2,0,1:T(8,128)}, u32[]{:S(2)}) copy-start(f32[5,2,1984]{2,0,1:T(8,128)} %get-tuple-element.118) | copy-start | bytes 238084
  51.9 33.3 %copy-start.21 = (f32[5,2,1984]{2,0,1:T(8,128)S(1)}, f32[5,2,1984]{2,0,1:T(8,128)}, u32[]{:S(2)}) copy-start(f32[5,2,1984]{2,0,1:T(8,128)} %get-tuple-element.119) | copy-start | bytes 238084
  51.9 33.3 %copy-start.22 = (f32[5,2,1984]{2,0,1:T(8,128)S(1)}, f32[5,2,1984]{2,0,1:T(8,128)}, u32[]{:S(2)}) copy-start(f32[5,2,1984]{2,0,1:T(8,128)} %get-tuple-element.192) | copy-start | bytes 238084
  51.9 33.3 %copy-start.23 = (f32[5,2,1984]{2,0,1:T(8,128)S(1)}, f32[5,2,1984]{2,0,1:T(8,128)}, u32[]{:S(2)}) copy-start(f32[5,2,1984]{2,0,1:T(8,128)} %get-tuple-element.193) | copy-start | bytes 238084
  65.9 19.1 %all-to-all-start.2 = ((f32[32,1,512]{2,1,0:T(1,128)}), f32[32,1,512]{2,1,0:T(1,128)S(1)}, u32[]{:S(2)}, u32[]{:S(2)}) async-start(f32[32,1,512]{2,1,0:T(1,128)} %broadcast_in_dim.20), calls=%async_computation.2 | async-start | bytes 131072 | tf_op jit(solution)/shard_map/all_to_all | solution.py:20
  85.6 9.7 %collective-permute-start.3 = (f32[3,5,2,2048]{3,1,2,0:T(8,128)S(1)}, f32[3,5,2,2048]{3,1,2,0:T(8,128)S(1)}, u32[]{:S(2)}, u32[]{:S(2)}) collective-permute-start(f32[3,5,2,2048]{3,1,2,0:T(8,128)S(1)} %pad_maximum_fusion.5), channel_id=1, source_target_pairs={{1,0},{2,1},{3,2},{4,3},{5,4},{6,5},{7,6},{8,7},{9,8},{10,9},{11,1... | collective-permute-start | bytes 737288 | tf_op jit(solution)/shard_map/ppermute | solution.py:40
  87.5 10.8 %collective-permute-start.2 = (f32[3,5,2,2048]{3,1,2,0:T(8,128)S(1)}, f32[3,5,2,2048]{3,1,2,0:T(8,128)S(1)}, u32[]{:S(2)}, u32[]{:S(2)}) collective-permute-start(f32[3,5,2,2048]{3,1,2,0:T(8,128)S(1)} %pad_maximum_fusion.5), channel_id=1, source_target_pairs={{0,1},{1,2},{2,3},{3,4},{4,5},{5,6},{6,7},{7,8},{8,9},{9,10},{10,1... | collective-permute-start | bytes 737288 | tf_op jit(solution)/shard_map/ppermute | solution.py:38
  109.6 19.8 %all-to-all-start.3 = ((f32[32,1,512]{2,1,0:T(1,128)}), f32[32,1,512]{2,1,0:T(1,128)}, u32[]{:S(2)}, u32[]{:S(2)}) async-start(f32[32,1,512]{2,1,0:T(1,128)} %all_to_all.48), calls=%async_computation.3 | async-start | bytes 131072 | tf_op jit(solution)/shard_map/all_to_all | solution.py:55
  116.0 34.4 %copy-start.8 = (f32[5,2,1984]{2,0,1:T(8,128)S(1)}, f32[5,2,1984]{2,0,1:T(8,128)}, u32[]{:S(2)}) copy-start(f32[5,2,1984]{2,0,1:T(8,128)} %get-tuple-element.110) | copy-start | bytes 238084
  116.0 34.4 %copy-start.9 = (f32[5,2,1984]{2,0,1:T(8,128)S(1)}, f32[5,2,1984]{2,0,1:T(8,128)}, u32[]{:S(2)}) copy-start(f32[5,2,1984]{2,0,1:T(8,128)} %get-tuple-element.111) | copy-start | bytes 238084
  116.0 34.4 %copy-start.16 = (f32[5,2,1984]{2,0,1:T(8,128)S(1)}, f32[5,2,1984]{2,0,1:T(8,128)}, u32[]{:S(2)}) copy-start(f32[5,2,1984]{2,0,1:T(8,128)} %get-tuple-element.178) | copy-start | bytes 238084
  116.0 34.4 %copy-start.17 = (f32[5,2,1984]{2,0,1:T(8,128)S(1)}, f32[5,2,1984]{2,0,1:T(8,128)}, u32[]{:S(2)}) copy-start(f32[5,2,1984]{2,0,1:T(8,128)} %get-tuple-element.179) | copy-start | bytes 238084
  116.0 34.4 %copy-start.26 = (f32[5,2,1920]{2,0,1:T(8,128)S(1)}, f32[5,2,1920]{2,0,1:T(8,128)}, u32[]{:S(2)}) copy-start(f32[5,2,1920]{2,0,1:T(8,128)} %get-tuple-element.106) | copy-start | bytes 230404
  116.1 34.4 %copy-start.27 = (f32[5,2,1920]{2,0,1:T(8,128)S(1)}, f32[5,2,1920]{2,0,1:T(8,128)}, u32[]{:S(2)}) copy-start(f32[5,2,1920]{2,0,1:T(8,128)} %get-tuple-element.107) | copy-start | bytes 230404
  131.0 19.1 %all-to-all-start.4 = ((f32[32,1,512]{2,1,0:T(1,128)}), f32[32,1,512]{2,1,0:T(1,128)S(1)}, u32[]{:S(2)}, u32[]{:S(2)}) async-start(f32[32,1,512]{2,1,0:T(1,128)} %broadcast_in_dim.22), calls=%async_computation.4 | async-start | bytes 131072 | tf_op jit(solution)/shard_map/all_to_all | solution.py:20
  150.7 8.8 %collective-permute-start.5 = (f32[3,5,2,2048]{3,1,2,0:T(8,128)S(1)}, f32[3,5,2,2048]{3,1,2,0:T(8,128)S(1)}, u32[]{:S(2)}, u32[]{:S(2)}) collective-permute-start(f32[3,5,2,2048]{3,1,2,0:T(8,128)S(1)} %pad_maximum_fusion.6), channel_id=1, source_target_pairs={{1,0},{2,1},{3,2},{4,3},{5,4},{6,5},{7,6},{8,7},{9,8},{10,9},{11,1... | collective-permute-start | bytes 737288 | tf_op jit(solution)/shard_map/ppermute | solution.py:40
  152.6 11.9 %collective-permute-start.4 = (f32[3,5,2,2048]{3,1,2,0:T(8,128)S(1)}, f32[3,5,2,2048]{3,1,2,0:T(8,128)S(1)}, u32[]{:S(2)}, u32[]{:S(2)}) collective-permute-start(f32[3,5,2,2048]{3,1,2,0:T(8,128)S(1)} %pad_maximum_fusion.6), channel_id=1, source_target_pairs={{0,1},{1,2},{2,3},{3,4},{4,5},{5,6},{6,7},{7,8},{8,9},{9,10},{10,1... | collective-permute-start | bytes 737288 | tf_op jit(solution)/shard_map/ppermute | solution.py:38
  175.9 19.8 %all-to-all-start.5 = ((f32[32,1,512]{2,1,0:T(1,128)}), f32[32,1,512]{2,1,0:T(1,128)}, u32[]{:S(2)}, u32[]{:S(2)}) async-start(f32[32,1,512]{2,1,0:T(1,128)} %all_to_all.51), calls=%async_computation.5 | async-start | bytes 131072 | tf_op jit(solution)/shard_map/all_to_all | solution.py:55
  182.5 34.1 %copy-start.10 = (f32[5,2,1984]{2,0,1:T(8,128)S(1)}, f32[5,2,1984]{2,0,1:T(8,128)}, u32[]{:S(2)}) copy-start(f32[5,2,1984]{2,0,1:T(8,128)} %get-tuple-element.102) | copy-start | bytes 238084
  182.5 34.1 %copy-start.11 = (f32[5,2,1984]{2,0,1:T(8,128)S(1)}, f32[5,2,1984]{2,0,1:T(8,128)}, u32[]{:S(2)}) copy-start(f32[5,2,1984]{2,0,1:T(8,128)} %get-tuple-element.103) | copy-start | bytes 238084
  182.5 34.1 %copy-start.18 = (f32[5,2,1984]{2,0,1:T(8,128)S(1)}, f32[5,2,1984]{2,0,1:T(8,128)}, u32[]{:S(2)}) copy-start(f32[5,2,1984]{2,0,1:T(8,128)} %get-tuple-element.174) | copy-start | bytes 238084
  182.5 34.1 %copy-start.19 = (f32[5,2,1984]{2,0,1:T(8,128)S(1)}, f32[5,2,1984]{2,0,1:T(8,128)}, u32[]{:S(2)}) copy-start(f32[5,2,1984]{2,0,1:T(8,128)} %get-tuple-element.175) | copy-start | bytes 238084
  182.6 34.1 %copy-start.28 = (f32[5,2,1920]{2,0,1:T(8,128)S(1)}, f32[5,2,1920]{2,0,1:T(8,128)}, u32[]{:S(2)}) copy-start(f32[5,2,1920]{2,0,1:T(8,128)} %get-tuple-element.98) | copy-start | bytes 230404
  182.6 34.1 %copy-start.29 = (f32[5,2,1920]{2,0,1:T(8,128)S(1)}, f32[5,2,1920]{2,0,1:T(8,128)}, u32[]{:S(2)}) copy-start(f32[5,2,1920]{2,0,1:T(8,128)} %get-tuple-element.99) | copy-start | bytes 230404
  197.3 19.0 %all-to-all-start.6 = ((f32[32,1,512]{2,1,0:T(1,128)}), f32[32,1,512]{2,1,0:T(1,128)S(1)}, u32[]{:S(2)}, u32[]{:S(2)}) async-start(f32[32,1,512]{2,1,0:T(1,128)} %broadcast_in_dim.24), calls=%async_computation.6 | async-start | bytes 131072 | tf_op jit(solution)/shard_map/all_to_all | solution.py:20
  217.0 9.7 %collective-permute-start.7 = (f32[3,5,2,2048]{3,1,2,0:T(8,128)S(1)}, f32[3,5,2,2048]{3,1,2,0:T(8,128)S(1)}, u32[]{:S(2)}, u32[]{:S(2)}) collective-permute-start(f32[3,5,2,2048]{3,1,2,0:T(8,128)S(1)} %pad_maximum_fusion.7), channel_id=1, source_target_pairs={{1,0},{2,1},{3,2},{4,3},{5,4},{6,5},{7,6},{8,7},{9,8},{10,9},{11,1... | collective-permute-start | bytes 737288 | tf_op jit(solution)/shard_map/ppermute | solution.py:40
  218.9 10.9 %collective-permute-start.6 = (f32[3,5,2,2048]{3,1,2,0:T(8,128)S(1)}, f32[3,5,2,2048]{3,1,2,0:T(8,128)S(1)}, u32[]{:S(2)}, u32[]{:S(2)}) collective-permute-start(f32[3,5,2,2048]{3,1,2,0:T(8,128)S(1)} %pad_maximum_fusion.7), channel_id=1, source_target_pairs={{0,1},{1,2},{2,3},{3,4},{4,5},{5,6},{6,7},{7,8},{8,9},{9,10},{10,1... | collective-permute-start | bytes 737288 | tf_op jit(solution)/shard_map/ppermute | solution.py:38
  242.1 19.8 %all-to-all-start.7 = ((f32[32,1,512]{2,1,0:T(1,128)}), f32[32,1,512]{2,1,0:T(1,128)}, u32[]{:S(2)}, u32[]{:S(2)}) async-start(f32[32,1,512]{2,1,0:T(1,128)} %all_to_all.54), calls=%async_computation.7 | async-start | bytes 131072 | tf_op jit(solution)/shard_map/all_to_all | solution.py:55
  248.6 34.2 %copy-start.6 = (f32[5,2,1984]{2,0,1:T(8,128)S(1)}, f32[5,2,1984]{2,0,1:T(8,128)}, u32[]{:S(2)}) copy-start(f32[5,2,1984]{2,0,1:T(8,128)} %get-tuple-element.94) | copy-start | bytes 238084
  248.6 34.2 %copy-start.7 = (f32[5,2,1984]{2,0,1:T(8,128)S(1)}, f32[5,2,1984]{2,0,1:T(8,128)}, u32[]{:S(2)}) copy-start(f32[5,2,1984]{2,0,1:T(8,128)} %get-tuple-element.95) | copy-start | bytes 238084
  248.7 34.2 %copy-start.14 = (f32[5,2,1984]{2,0,1:T(8,128)S(1)}, f32[5,2,1984]{2,0,1:T(8,128)}, u32[]{:S(2)}) copy-start(f32[5,2,1984]{2,0,1:T(8,128)} %get-tuple-element.170) | copy-start | bytes 238084
  248.7 34.2 %copy-start.15 = (f32[5,2,1984]{2,0,1:T(8,128)S(1)}, f32[5,2,1984]{2,0,1:T(8,128)}, u32[]{:S(2)}) copy-start(f32[5,2,1984]{2,0,1:T(8,128)} %get-tuple-element.171) | copy-start | bytes 238084
  248.7 34.2 %copy-start.24 = (f32[5,2,1920]{2,0,1:T(8,128)S(1)}, f32[5,2,1920]{2,0,1:T(8,128)}, u32[]{:S(2)}) copy-start(f32[5,2,1920]{2,0,1:T(8,128)} %get-tuple-element.90) | copy-start | bytes 230404
  248.7 34.2 %copy-start.25 = (f32[5,2,1920]{2,0,1:T(8,128)S(1)}, f32[5,2,1920]{2,0,1:T(8,128)}, u32[]{:S(2)}) copy-start(f32[5,2,1920]{2,0,1:T(8,128)} %get-tuple-element.91) | copy-start | bytes 230404
  263.4 19.1 %all-to-all-start.8 = ((f32[32,1,512]{2,1,0:T(1,128)}), f32[32,1,512]{2,1,0:T(1,128)S(1)}, u32[]{:S(2)}, u32[]{:S(2)}) async-start(f32[32,1,512]{2,1,0:T(1,128)} %broadcast_in_dim.26), calls=%async_computation.8 | async-start | bytes 131072 | tf_op jit(solution)/shard_map/all_to_all | solution.py:20
  (4 other events, 21.3 us)
where the time goes:
time: 285 us; the launch traced here: 284 us
  waiting for transfers between devices  138 us (48%)
  starting transfers between devices  71.9 us (25%)
  local copies, waits for them, and re-layouts  35.7 us (13%)
  other arithmetic  25.9 us (9%)
  matrix products  8.32 us (3%)
  between operations  3.52 us (1%)
    all_to_all x5, waiting for transfers between devices, from_everyone(): lax.all_to_all(jnp.broadcast_to(shard[None], (count, *shard.shape)), axis...  60.6 us
    all_to_all x4, waiting for transfers between devices, sum_at_owner(): lax.all_to_all(parts, axis, split_axis=0, concat_axis=0, tiled=True)  51.7 us
    all_to_all x4, starting transfers between devices, sum_at_owner(): lax.all_to_all(parts, axis, split_axis=0, concat_axis=0, tiled=True)  30 us
    all_to_all x5, starting transfers between devices, from_everyone(): lax.all_to_all(jnp.broadcast_to(shard[None], (count, *shard.shape)), axis...  24.1 us
    ppermute x4, waiting for transfers between devices, with_halo(): lax.ppermute(head, axis, [((i + 1) % count, i) for i in range(ends)])  15 us
    ppermute x4, waiting for transfers between devices, with_halo(): lax.ppermute(tail, axis, [(i, (i + 1) % count) for i in range(ends)])  11.2 us
    slice x16, local copies, waits for them, and re-layouts, fourth_across(): jnp.roll(values, NZ, axis=-1)  9.85 us
    ppermute x4, starting transfers between devices, with_halo(): lax.ppermute(tail, axis, [(i, (i + 1) % count) for i in range(ends)])  9.32 us
  transfers between devices with their start and end apart: 17, of which 15 were waited for; matrix products, arithmetic and copies ran while one was open for 5% of the time, Pallas kernels for 0%

commit v1 on v0

v1 whole, which is shorter than its diff:
```python
import functools

import jax
import jax.numpy as jnp
from jax import lax
from jax.experimental import pallas as pl
from jax.experimental.pallas import tpu as pltpu
from jax.sharding import PartitionSpec as P

NZ = 64
EPS_FOURTH = 0.05
COURANT = 0.9
OMEGA_BASE = 0.25
WALL_RATE = 2.0
HUB_RADIUS = 0.5
SECTION_RATES = (0.25, 1.0 / 3.0, 0.5, 1.0)
STRESS_PAIRS = ((1, 1), (1, 2), (1, 3), (2, 2), (2, 3), (3, 3), (4, 1), (4, 2), (4, 3))

VARS = 5
CELLS = 2
C1 = 16
LANES = 128
H_ROWS = 2 * VARS * CELLS * C1
M_ROWS = VARS * CELLS * C1
W_ROWS = CELLS * C1


def h_row(part, var, cell):
    return ((part * VARS + var) * CELLS + cell) * C1


def m_row(var, cell):
    return (var * CELLS + cell) * C1


def pack_kernel(harm_ref, freq_ref, out_ref, rows_ref):
    for part in range(2):
        for var in range(VARS):
            for cell in range(CELLS):
                for c1 in range(C1):
                    row = h_row(part, var, cell) + c1
                    rows_ref[row : row + 1, :] = harm_ref[
                        0, part, var, cell : cell + 1, c1 * LANES : (c1 + 1) * LANES
                    ]
    omega = OMEGA_BASE * freq_ref[0].astype(jnp.float32)
    rows_ref[H_ROWS:, :] = jnp.full((rows_ref.shape[0] - H_ROWS, LANES), omega, jnp.float32)
    turned = rows_ref[...].T
    for j in range(32):
        out_ref[j, 0:2, :] = turned[2 * j : 2 * j + 2, :]
        out_ref[j, 2:4, :] = turned[NZ + 2 * j : NZ + 2 * j + 2, :]


def pack_mean(tiles):
    group = lax.broadcasted_iota(jnp.int32, (8, LANES), 1) // 4
    packed = jnp.zeros((8, LANES), jnp.float32)
    for i, tile in enumerate(tiles):
        for half in range(2):
            packed = jnp.where(group == 2 * i + half, tile[8 * half : 8 * half + 8, :], packed)
    return packed


def unpack_mean(packed):
    lane = lax.broadcasted_iota(jnp.int32, (8, LANES), 1) % 4
    tiles = []
    for i in range(VARS * CELLS):
        halves = [
            jnp.take_along_axis(packed, lane + 4 * (2 * i + half), axis=1) for half in range(2)
        ]
        tiles.append(jnp.concatenate(halves, axis=0))
    return tiles


def prepare_kernel(mean_ref, wall_ref, position_ref, mean_out, wall_out, packed_out, rows_ref):
    for cell in range(CELLS):
        for c1 in range(C1):
            cols = slice(c1 * LANES, (c1 + 1) * LANES)
            for var in range(VARS):
                row = m_row(var, cell) + c1
                rows_ref[row : row + 1, :] = mean_ref[var, cell : cell + 1, cols]
            row = M_ROWS + cell * C1 + c1
            rows_ref[row : row + 1, :] = wall_ref[cell : cell + 1, cols].astype(jnp.float32)
    lane = lax.broadcasted_iota(jnp.int32, (8, LANES), 1)
    source = ((lane // 2) % 2) * NZ + 2 * position_ref[0] + lane % 2
    for start in range(0, M_ROWS + W_ROWS, 8):
        picked = jnp.take_along_axis(rows_ref[start : start + 8, :], source, axis=1)
        if start < M_ROWS:
            mean_out[start : start + 8, :] = picked
        else:
            wall_out[start - M_ROWS : start - M_ROWS + 8, :] = picked
    packed_out[...] = pack_mean(
        [mean_out[i * C1 : (i + 1) * C1, :] for i in range(VARS * CELLS)]
    )


def unpack_kernel(arrived_ref, packed_ref, state_out, omega_out, rows_ref):
    for k in range(32):
        rows_ref[4 * k : 4 * k + 4, :] = arrived_ref[k]
    turned = rows_ref[...].T
    state_out[:H_ROWS, :] = turned[:H_ROWS, :]
    state_out[H_ROWS:, :] = packed_ref[...]
    omega_out[...] = turned[H_ROWS : H_ROWS + 8, :]


def section_kernel(
    own_ref, left_ref, right_ref, h0_ref, m0_ref, mean_ref, omega_ref, wall_ref, jac_ref,
    step_ref, radius_ref, *outs, rate, last
):
    lane = lax.broadcasted_iota(jnp.int32, (C1, LANES), 1)
    even = (lane // 2) % 2 == 0

    def up(tile):
        return pltpu.roll(tile, C1 - 1, 0)

    def down(tile):
        return pltpu.roll(tile, 1, 0)

    def beside(tile):
        swapped = jnp.where(even, pltpu.roll(tile, LANES - 2, 1), pltpu.roll(tile, 2, 1))
        return jnp.where(even, swapped, up(swapped)), jnp.where(even, down(swapped), swapped)

    def splat(ref, row):
        return jnp.broadcast_to(ref[row : row + 1, :], (C1, LANES))

    def apply_matrix(base, tiles):
        out = []
        for a in range(VARS):
            total = splat(jac_ref, base + VARS * a) * tiles[0]
            for b in range(1, VARS):
                total = total + splat(jac_ref, base + VARS * a + b) * tiles[b]
            out.append(total)
        return out

    def column(part, var):
        row = h_row(part, var, 0)
        return [
            ref[row + C1 * cell : row + C1 * (cell + 1), :]
            for ref in (left_ref, own_ref, right_ref)
            for cell in range(CELLS)
        ]

    omega = splat(omega_ref, 0)
    step = rate * splat(step_ref, 0)
    inv_radius = 1.0 / splat(radius_ref, 0)

    harm = [[column(part, var) for var in range(VARS)] for part in range(2)]
    left_mean = unpack_mean(left_ref[H_ROWS:, :])
    right_mean = unpack_mean(right_ref[H_ROWS:, :])
    mean = []
    for var in range(VARS):
        own_mean = [
            mean_ref[m_row(var, cell) : m_row(var, cell) + C1, :] for cell in range(CELLS)
        ]
        mean.append(
            left_mean[CELLS * var : CELLS * (var + 1)]
            + own_mean
            + right_mean[CELLS * var : CELLS * (var + 1)]
        )

    def smooth_parts(cells, at):
        center = cells[at]
        above, below = beside(center)
        diff_y = (above - below) * 0.5
        fourth = (
            (cells[at + 2] + cells[at - 2])
            + (up(center) + down(center))
            - 4.0 * ((cells[at + 1] + cells[at - 1]) + (above + below))
            + 12.0 * center
        )
        return diff_y, fourth

    harm_new = {}
    for cell in range(CELLS):
        at = 2 + cell
        wall = WALL_RATE * wall_ref[cell * C1 : (cell + 1) * C1, :]
        for part in range(2):
            diffs_x, diffs_y, fourths = [], [], []
            for var in range(VARS):
                cells = harm[part][var]
                diffs_x.append(
                    (mean[1][at + 1] * cells[at + 1] - mean[1][at - 1] * cells[at - 1]) * 0.5
                )
                diff_y, fourth = smooth_parts(cells, at)
                diffs_y.append(diff_y)
                fourths.append(fourth)
            flux_x = apply_matrix(0, diffs_x)
            flux_y = apply_matrix(VARS * VARS, diffs_y)
            for var in range(VARS):
                turned = omega * harm[1 - part][var][at]
                if part:
                    turned = -turned
                res = (
                    turned
                    - flux_x[var]
                    - flux_y[var]
                    - EPS_FOURTH * fourths[var]
                    - wall * harm[part][var][at]
                )
                row = h_row(part, var, cell)
                harm_new[part, var, cell] = h0_ref[row : row + C1, :] + step * res

    def stress(index, at):
        a, b = STRESS_PAIRS[index]
        return 0.5 * (harm[0][a][at] * harm[0][b][at] + harm[1][a][at] * harm[1][b][at])

    def total(tile):
        for shift in (4, 8, 16, 32, 64):
            tile = tile + pltpu.roll(tile, shift, 1)
        return jnp.take_along_axis(tile, lane % 4, axis=1)

    mean_new = {}
    for cell in range(CELLS):
        at = 2 + cell

        def grad_x(index):
            return (stress(index, at + 1) - stress(index, at - 1)) * 0.5

        def grad_y(tile):
            above, below = beside(tile)
            return (above - below) * 0.5

        s3, s4 = stress(3, at), stress(4, at)
        terms = [
            None,
            total(-grad_x(0) - grad_y(stress(1, at))),
            total(-grad_x(1) - grad_y(s3) - 2.0 * s4 * inv_radius),
            total(-grad_x(2) - grad_y(s4) + (s3 - stress(5, at)) * inv_radius),
            total(-grad_x(6) - grad_y(stress(7, at)) - stress(8, at) * inv_radius),
        ]
        diffs_x, diffs_y, fourths = [], [], []
        for var in range(VARS):
            cells = mean[var]
            diffs_x.append((cells[at + 1] - cells[at - 1]) * 0.5)
            diff_y, fourth = smooth_parts(cells, at)
            diffs_y.append(diff_y)
            fourths.append(fourth)
        flux_x = apply_matrix(0, diffs_x)
        flux_y = apply_matrix(VARS * VARS, diffs_y)
        for var in range(VARS):
            res = -flux_x[var] - flux_y[var] - EPS_FOURTH * fourths[var]
            if var:
                res = res + terms[var]
            row = m_row(var, cell)
            mean_new[var, cell] = m0_ref[row : row + C1, :] + step * res

    if last:
        out_ref, rows_ref = outs
        target, offset = rows_ref, H_ROWS
    else:
        state_out, mean_out = outs
        target, offset = state_out, None
    for (part, var, cell), tile in harm_new.items():
        row = h_row(part, var, cell)
        target[row : row + C1, :] = tile
    for (var, cell), tile in mean_new.items():
        row = m_row(var, cell)
        if last:
            target[offset + row : offset + row + C1, :] = tile
        else:
            mean_out[row : row + C1, :] = tile
    if last:
        spare = H_ROWS + M_ROWS
        rows_ref[spare:, :] = jnp.zeros((rows_ref.shape[0] - spare, LANES), jnp.float32)
        turned = rows_ref[...].T
        for k in range(32):
            out_ref[k] = turned[4 * k : 4 * k + 4, :]
    else:
        state_out[H_ROWS:, :] = pack_mean(
            [mean_new[var, cell] for var in range(VARS) for cell in range(CELLS)]
        )


def restore_kernel(arrived_ref, mean_out, harm_out, rows_ref):
    for j in range(32):
        rows_ref[2 * j : 2 * j + 2, :] = arrived_ref[j, 0:2, :]
        rows_ref[NZ + 2 * j : NZ + 2 * j + 2, :] = arrived_ref[j, 2:4, :]
    turned = rows_ref[...].T
    for var in range(VARS):
        for cell in range(CELLS):
            for c1 in range(C1):
                cols = slice(c1 * LANES, (c1 + 1) * LANES)
                for part in range(2):
                    row = h_row(part, var, cell) + c1
                    harm_out[0, part, var, cell : cell + 1, cols] = turned[row : row + 1, :]
                row = H_ROWS + m_row(var, cell) + c1
                mean_out[var, cell : cell + 1, cols] = turned[row : row + 1, :]


def f32(*shape):
    return jax.ShapeDtypeStruct(shape, jnp.float32)


VMEM = pl.BlockSpec(memory_space=pltpu.VMEM)
SMEM = pl.BlockSpec(memory_space=pltpu.SMEM)


def rows_scratch(*shape):
    return [pltpu.VMEM(shape, jnp.float32)]


def shards(harmonics, mean_flow, freq_index, wall_mask, jacobian_x, jacobian_y):
    plane_count = mean_flow.shape[2]
    slab_count = lax.axis_size("slab")
    position = lax.axis_index("harm")

    sends = pl.pallas_call(
        pack_kernel,
        out_shape=f32(32, 4, 384),
        in_specs=[VMEM, SMEM],
        out_specs=VMEM,
        scratch_shapes=rows_scratch(384, LANES),
        name="pack",
    )(harmonics, freq_index)
    arrived = lax.all_to_all(sends, "harm", 0, 0, tiled=True)

    speed = jnp.sum(mean_flow[1] * mean_flow[1])
    speeds = lax.all_to_all(
        jnp.broadcast_to(speed, (slab_count, 1, LANES)), "slab", 0, 0, tiled=True
    )
    speed_total = jnp.sum(speeds, axis=0)
    cell_count = CELLS * slab_count * plane_count
    step = COURANT / (1.0 + jnp.sqrt(speed_total / cell_count))

    mean_start, wall, packed = pl.pallas_call(
        prepare_kernel,
        out_shape=(f32(M_ROWS, LANES), f32(W_ROWS, LANES), f32(8, LANES)),
        in_specs=[VMEM, VMEM, SMEM],
        out_specs=(VMEM, VMEM, VMEM),
        scratch_shapes=rows_scratch(M_ROWS + W_ROWS, LANES),
        name="prepare",
    )(mean_flow, wall_mask, position.astype(jnp.int32).reshape(1))
    radial = 2 * position + jnp.arange(LANES) % 2
    radius = (HUB_RADIUS + (radial.astype(jnp.float32) + 0.5) / NZ).reshape(1, LANES)
    jac = jnp.concatenate([jacobian_x.reshape(-1, 1), jacobian_y.reshape(-1, 1)])
    jac = jnp.broadcast_to(jac, (2 * VARS * VARS, LANES))

    state, omega = pl.pallas_call(
        unpack_kernel,
        out_shape=(f32(H_ROWS + 8, LANES), f32(8, LANES)),
        in_specs=[VMEM, VMEM],
        out_specs=(VMEM, VMEM),
        scratch_shapes=rows_scratch(LANES, 384),
        name="unpack",
    )(arrived, packed)

    start, mean_now = state, mean_start
    for index, rate in enumerate(SECTION_RATES):
        last = index == len(SECTION_RATES) - 1
        left = lax.ppermute(state, "slab", [(i, i + 1) for i in range(slab_count - 1)])
        right = lax.ppermute(state, "slab", [(i + 1, i) for i in range(slab_count - 1)])
        if last:
            shapes, scratch = f32(32, 4, 512), rows_scratch(512, LANES)
            specs = VMEM
        else:
            shapes, scratch = (f32(H_ROWS + 8, LANES), f32(M_ROWS, LANES)), []
            specs = (VMEM, VMEM)
        result = pl.pallas_call(
            functools.partial(section_kernel, rate=rate, last=last),
            out_shape=shapes,
            in_specs=[VMEM] * 11,
            out_specs=specs,
            scratch_shapes=scratch,
            name=f"section{index}",
        )(state, left, right, start, mean_start, mean_now, omega, wall, jac, step, radius)
        if not last:
            state, mean_now = result
    back = lax.all_to_all(result, "harm", 0, 0, tiled=True)
    return pl.pallas_call(
        restore_kernel,
        out_shape=(f32(*mean_flow.shape), f32(*harmonics.shape)),
        in_specs=[VMEM],
        out_specs=(VMEM, VMEM),
        scratch_shapes=rows_scratch(LANES, 512),
        name="restore",
    )(back)


def solution(mesh):
    placed = (
        P("harm", None, None, "slab", None),
        P(None, "slab", None),
        P("harm"),
        P("slab", None),
        P(),
        P(),
    )
    return jax.shard_map(
        shards,
        mesh=mesh,
        in_specs=placed,
        out_specs=(P(None, "slab", None), P("harm", None, None, "slab", None)),
        check_vma=False,
    )
```

time: 285 us -> 133 us (0.47)
  the two profiles are of different devices: /device:TPU:16 before, /device:TPU:7 now
where the time goes in v1:
time: 133 us; the launch traced here: 132 us
  starting transfers between devices  52.7 us (40%)
  blocking collectives  26.4 us (20%)
  waiting for transfers between devices  25.8 us (19%)
  Pallas kernels  17.9 us (13%)
  local copies, waits for them, and re-layouts  5.42 us (4%)
  other arithmetic  2.57 us (2%)
  between operations  1.4 us (1%)
    all_to_all x1, blocking collectives, shards(): back = lax.all_to_all(result, 'harm', 0, 0, tiled=True)  26.4 us
    all_to_all x1, starting transfers between devices, shards(): arrived = lax.all_to_all(sends, 'harm', 0, 0, tiled=True)  17.7 us
    ppermute x4, starting transfers between devices, shards(): lax.ppermute(state, 'slab', [(i, i + 1) for i in range(slab_count - 1)])  16.8 us
    all_to_all x1, waiting for transfers between devices, shards(): arrived = lax.all_to_all(sends, 'harm', 0, 0, tiled=True)  14.1 us
    ppermute x4, starting transfers between devices, shards(): lax.ppermute(state, 'slab', [(i + 1, i) for i in range(slab_count - 1)])  12.1 us
    pallas_call x4, Pallas kernels, shards(): pl.pallas_call(functools.partial(section_kernel, rate=rate, last=last), o...  10.8 us
    all_to_all x1, starting transfers between devices, shards(): lax.all_to_all(jnp.broadcast_to(speed, (slab_count, 1, LANES)), 'slab', 0...  6.23 us
    ppermute x4, waiting for transfers between devices, shards(): lax.ppermute(state, 'slab', [(i, i + 1) for i in range(slab_count - 1)])  4.96 us
  transfers between devices with their start and end apart: 10, of which 10 were waited for; matrix products, arithmetic and copies ran while one was open for 1% of the time, Pallas kernels for 3%

profile of v1, /device:TPU:7, one launch (start us, length us, event | category | flops | bytes accessed | tf_op | source)
XLA Modules:
  0.0 132.3 jit_solution(11234874624836521696)
XLA Ops:
  0.6 1.3 %multiply_reduce_fusion = f32[]{:T(128)} fusion(f32[5,2,2048]{2,1,0:T(2,128)} %mean_ref.1), kind=kLoop, calls=%fused_computation | loop fusion | flops 8191 | bytes 16388 | tf_op jit(solution)/shard_map/reduce_sum | solution.py:315
  2.0 1.2 broadcast_in_dim.12
  3.2 6.2 %all-to-all-start.1 = ((f32[16,1,128]{2,1,0:T(1,128)}), f32[16,1,128]{2,1,0:T(1,128)S(1)}, u32[]{:S(2)}, u32[]{:S(2)}) async-start(f32[16,1,128]{2,1,0:T(1,128)} %broadcast_in_dim.12), calls=%async_computation.1 | async-start | bytes 16384 | tf_op jit(solution)/shard_map/all_to_all | solution.py:316
  10.1 1.8 %pack.1 = f32[32,4,384]{2,1,0:T(4,128)} custom-call(f32[1,2,5,2,2048]{4,3,2,1,0:T(2,128)} %harm_ref.1, s32[1]{0:T(128)S(6)} %copy.9.freq_ref), custom_call_target="tpu_custom_call" | custom-call | tf_op jit(solution)/shard_map/pack/pallas_call | solution.py:305
  11.9 1.9 %all-to-all-done.1 = f32[16,1,128]{2,1,0:T(1,128)S(1)} async-done(((f32[16,1,128]{2,1,0:T(1,128)}), f32[16,1,128]{2,1,0:T(1,128)S(1)}, u32[]{:S(2)}, u32[]{:S(2)}) %all-to-all-start.1) | async-done | bytes 8224 | tf_op jit(solution)/shard_map/all_to_all | solution.py:316
  13.8 17.7 %all-to-all-start = ((f32[32,4,384]{2,1,0:T(4,128)}), f32[32,4,384]{2,1,0:T(4,128)S(1)}, u32[]{:S(2)}, u32[]{:S(2)}) async-start(f32[32,4,384]{2,1,0:T(4,128)} %pack.1), calls=%async_computation | async-start | bytes 393216 | tf_op jit(solution)/shard_map/all_to_all | solution.py:313
  31.5 0.0 copy-start.9
  31.5 0.0 copy-start.10
  31.5 0.7 copy-done.9
  32.2 0.1 reshape.81
  32.3 0.0 copy-done.10
  32.3 0.1 reshape.82
  32.3 1.7 %prepare.1 = (f32[160,128]{1,0:T(8,128)}, f32[32,128]{1,0:T(8,128)}, f32[8,128]{1,0:T(8,128)}) custom-call(f32[5,2,2048]{2,1,0:T(2,128)} %mean_ref.1, s32[2,2048]{1,0:T(2,128)} %wall_ref.1, s32[1]{0:T(128)} %bitcast.position_ref), custom_call_target="tpu_custom_call" | custom-call | tf_op jit(solution)/shard_map/prepare/pallas_call | solution.py:323
  34.0 0.6 fusion.4.radius_ref
  34.6 0.1 maximum_bitcast_fusion
  34.7 14.1 %all-to-all-done.arrived_ref = f32[32,4,384]{2,1,0:T(4,128)S(1)} async-done(((f32[32,4,384]{2,1,0:T(4,128)}), f32[32,4,384]{2,1,0:T(4,128)S(1)}, u32[]{:S(2)}, u32[]{:S(2)}) %all-to-all-start) | async-done | bytes 196640 | tf_op jit(solution)/shard_map/all_to_all | solution.py:313
  48.8 0.7 copy-done
  49.4 1.7 %unpack.1 = (f32[328,128]{1,0:T(8,128)}, f32[8,128]{1,0:T(8,128)}) custom-call(f32[32,4,384]{2,1,0:T(4,128)} %copy-done, f32[8,128]{1,0:T(8,128)} %get-tuple-element.13.packed_ref), custom_call_target="tpu_custom_call" | custom-call | tf_op jit(solution)/shard_map/unpack/pallas_call | solution.py:336
  51.2 4.6 %collective-permute-start.1 = (f32[328,128]{1,0:T(8,128)}, f32[328,128]{1,0:T(8,128)S(1)}, u32[]{:S(2)}, u32[]{:S(2)}) collective-permute-start(f32[328,128]{1,0:T(8,128)} %get-tuple-element.14.own_ref.h0_ref), channel_id=1, source_target_pairs={{1,0},{2,1},{3,2},{4,3},{5,4},{6,5},{7,6},{8,7},{9,8},{10,9},{11,1... | collective-permute-start | bytes 503816 | tf_op jit(solution)/shard_map/ppermute | solution.py:349
  55.8 3.0 %collective-permute-start = (f32[328,128]{1,0:T(8,128)}, f32[328,128]{1,0:T(8,128)S(1)}, u32[]{:S(2)}, u32[]{:S(2)}) collective-permute-start(f32[328,128]{1,0:T(8,128)} %get-tuple-element.14.own_ref.h0_ref), channel_id=1, source_target_pairs={{0,1},{1,2},{2,3},{3,4},{4,5},{5,6},{6,7},{7,8},{8,9},{9,10},{10,1... | collective-permute-start | bytes 503816 | tf_op jit(solution)/shard_map/ppermute | solution.py:348
  58.8 0.5 divide_bitcast_fusion.step_ref
  59.3 0.8 collective-permute-done.1.right_ref
  60.1 1.3 collective-permute-done.left_ref
  61.4 0.7 broadcast_in_dim.11.jac_ref
  62.1 0.0 copy-done.1
  62.1 2.6 %section0.1 = (f32[328,128]{1,0:T(8,128)}, f32[160,128]{1,0:T(8,128)}) custom-call(f32[328,128]{1,0:T(8,128)} %get-tuple-element.14.own_ref.h0_ref, f32[328,128]{1,0:T(8,128)} %copy-done.2, f32[328,128]{1,0:T(8,128)} %copy-done.1, f32[328,128]{1,0:T(8,128)} %get-tuple-element.14.own_ref.h0_ref, f32[160,128]{1,0:T(8,128)} %get-tuple-element.15.m0_ref.mean_ref, ...), custom_call_target="tpu_custom_call" | custom-call | tf_op jit(solution)/shard_map/section0/pallas_call | solution.py:356
  64.7 3.2 %collective-permute-start.3 = (f32[328,128]{1,0:T(8,128)}, f32[328,128]{1,0:T(8,128)S(1)}, u32[]{:S(2)}, u32[]{:S(2)}) collective-permute-start(f32[328,128]{1,0:T(8,128)} %get-tuple-element.18.own_ref), channel_id=1, source_target_pairs={{1,0},{2,1},{3,2},{4,3},{5,4},{6,5},{7,6},{8,7},{9,8},{10,9},{11,1... | collective-permute-start | bytes 503816 | tf_op jit(solution)/shard_map/ppermute | solution.py:349
  67.9 3.9 %collective-permute-start.2 = (f32[328,128]{1,0:T(8,128)}, f32[328,128]{1,0:T(8,128)S(1)}, u32[]{:S(2)}, u32[]{:S(2)}) collective-permute-start(f32[328,128]{1,0:T(8,128)} %get-tuple-element.18.own_ref), channel_id=1, source_target_pairs={{0,1},{1,2},{2,3},{3,4},{4,5},{5,6},{6,7},{7,8},{8,9},{9,10},{10,1... | collective-permute-start | bytes 503816 | tf_op jit(solution)/shard_map/ppermute | solution.py:348
  71.8 1.4 %collective-permute-done.3.right_ref = f32[328,128]{1,0:T(8,128)S(1)} collective-permute-done((f32[328,128]{1,0:T(8,128)}, f32[328,128]{1,0:T(8,128)S(1)}, u32[]{:S(2)}, u32[]{:S(2)}) %collective-permute-start.3) | collective-permute-done | bytes 167968 | tf_op jit(solution)/shard_map/ppermute | solution.py:349
  73.2 1.2 collective-permute-done.2.left_ref
  74.4 0.0 copy-done.3
  74.4 0.7 copy-done.5
  75.1 2.6 %section1.1 = (f32[328,128]{1,0:T(8,128)}, f32[160,128]{1,0:T(8,128)}) custom-call(f32[328,128]{1,0:T(8,128)} %get-tuple-element.18.own_ref, f32[328,128]{1,0:T(8,128)} %copy-done.5, f32[328,128]{1,0:T(8,128)} %copy-done.3, f32[328,128]{1,0:T(8,128)} %get-tuple-element.14.own_ref.h0_ref, f32[160,128]{1,0:T(8,128)} %get-tuple-element.15.m0_ref.mean_ref, ...), custom_call_target="tpu_custom_call" | custom-call | tf_op jit(solution)/shard_map/section1/pallas_call | solution.py:356
  77.7 2.3 %collective-permute-start.5 = (f32[328,128]{1,0:T(8,128)}, f32[328,128]{1,0:T(8,128)S(1)}, u32[]{:S(2)}, u32[]{:S(2)}) collective-permute-start(f32[328,128]{1,0:T(8,128)} %get-tuple-element.20.own_ref), channel_id=1, source_target_pairs={{1,0},{2,1},{3,2},{4,3},{5,4},{6,5},{7,6},{8,7},{9,8},{10,9},{11,1... | collective-permute-start | bytes 503816 | tf_op jit(solution)/shard_map/ppermute | solution.py:349
  80.0 4.8 %collective-permute-start.4 = (f32[328,128]{1,0:T(8,128)}, f32[328,128]{1,0:T(8,128)S(1)}, u32[]{:S(2)}, u32[]{:S(2)}) collective-permute-start(f32[328,128]{1,0:T(8,128)} %get-tuple-element.20.own_ref), channel_id=1, source_target_pairs={{0,1},{1,2},{2,3},{3,4},{4,5},{5,6},{6,7},{7,8},{8,9},{9,10},{10,1... | collective-permute-start | bytes 503816 | tf_op jit(solution)/shard_map/ppermute | solution.py:348
  84.8 1.4 %collective-permute-done.5.right_ref = f32[328,128]{1,0:T(8,128)S(1)} collective-permute-done((f32[328,128]{1,0:T(8,128)}, f32[328,128]{1,0:T(8,128)S(1)}, u32[]{:S(2)}, u32[]{:S(2)}) %collective-permute-start.5) | collective-permute-done | bytes 167968 | tf_op jit(solution)/shard_map/ppermute | solution.py:349
  86.2 1.2 collective-permute-done.4.left_ref
  87.4 0.0 copy-done.4
  87.4 0.7 copy-done.6
  88.1 2.6 %section2.1 = (f32[328,128]{1,0:T(8,128)}, f32[160,128]{1,0:T(8,128)}) custom-call(f32[328,128]{1,0:T(8,128)} %get-tuple-element.20.own_ref, f32[328,128]{1,0:T(8,128)} %copy-done.6, f32[328,128]{1,0:T(8,128)} %copy-done.4, f32[328,128]{1,0:T(8,128)} %get-tuple-element.14.own_ref.h0_ref, f32[160,128]{1,0:T(8,128)} %get-tuple-element.15.m0_ref.mean_ref, ...), custom_call_target="tpu_custom_call" | custom-call | tf_op jit(solution)/shard_map/section2/pallas_call | solution.py:356
  90.7 1.9 %collective-permute-start.7 = (f32[328,128]{1,0:T(8,128)}, f32[328,128]{1,0:T(8,128)S(1)}, u32[]{:S(2)}, u32[]{:S(2)}) collective-permute-start(f32[328,128]{1,0:T(8,128)} %get-tuple-element.22.own_ref), channel_id=1, source_target_pairs={{1,0},{2,1},{3,2},{4,3},{5,4},{6,5},{7,6},{8,7},{9,8},{10,9},{11,1... | collective-permute-start | bytes 503816 | tf_op jit(solution)/shard_map/ppermute | solution.py:349
  92.6 5.2 %collective-permute-start.6 = (f32[328,128]{1,0:T(8,128)}, f32[328,128]{1,0:T(8,128)S(1)}, u32[]{:S(2)}, u32[]{:S(2)}) collective-permute-start(f32[328,128]{1,0:T(8,128)} %get-tuple-element.22.own_ref), channel_id=1, source_target_pairs={{0,1},{1,2},{2,3},{3,4},{4,5},{5,6},{6,7},{7,8},{8,9},{9,10},{10,1... | collective-permute-start | bytes 503816 | tf_op jit(solution)/shard_map/ppermute | solution.py:348
  97.8 1.4 %collective-permute-done.7.right_ref = f32[328,128]{1,0:T(8,128)S(1)} collective-permute-done((f32[328,128]{1,0:T(8,128)}, f32[328,128]{1,0:T(8,128)S(1)}, u32[]{:S(2)}, u32[]{:S(2)}) %collective-permute-start.7) | collective-permute-done | bytes 167968 | tf_op jit(solution)/shard_map/ppermute | solution.py:349
  99.2 1.2 collective-permute-done.6.left_ref
  100.4 0.7 copy-done.8
  101.1 2.9 %section3.1 = f32[32,4,512]{2,1,0:T(4,128)} custom-call(f32[328,128]{1,0:T(8,128)} %get-tuple-element.22.own_ref, f32[328,128]{1,0:T(8,128)} %copy-done.8, f32[328,128]{1,0:T(8,128)} %copy-done.7, f32[328,128]{1,0:T(8,128)} %get-tuple-element.14.own_ref.h0_ref, f32[160,128]{1,0:T(8,128)} %get-tuple-element.15.m0_ref.mean_ref, ...), custom_call_target="tpu_custom_call" | custom-call | tf_op jit(solution)/shard_map/section3/pallas_call | solution.py:356
  104.0 26.4 %all_to_all.15.arrived_ref = f32[32,4,512]{2,1,0:T(4,128)} all-to-all(f32[32,4,512]{2,1,0:T(4,128)} %section3.1), channel_id=1, replica_groups=mesh['harm'=32,'slab'=16] {'harm'}, dimensions={0} | all-to-all | bytes 524288 | tf_op jit(solution)/shard_map/all_to_all | solution.py:366
  130.4 1.8 %restore.1 = (f32[5,2,2048]{2,1,0:T(2,128)}, f32[1,2,5,2,2048]{4,3,2,1,0:T(2,128)}) custom-call(f32[32,4,512]{2,1,0:T(4,128)} %all_to_all.15.arrived_ref), custom_call_target="tpu_custom_call" | custom-call | tf_op jit(solution)/shard_map/restore/pallas_call | solution.py:367
  (12 shorter events, 0.0 us)
Async XLA Ops:
  3.2 10.6 %all-to-all-start.1 = ((f32[16,1,128]{2,1,0:T(1,128)}), f32[16,1,128]{2,1,0:T(1,128)S(1)}, u32[]{:S(2)}, u32[]{:S(2)}) async-start(f32[16,1,128]{2,1,0:T(1,128)} %broadcast_in_dim.12), calls=%async_computation.1 | async-start | bytes 16384 | tf_op jit(solution)/shard_map/all_to_all | solution.py:316
  13.8 34.9 %all-to-all-start = ((f32[32,4,384]{2,1,0:T(4,128)}), f32[32,4,384]{2,1,0:T(4,128)S(1)}, u32[]{:S(2)}, u32[]{:S(2)}) async-start(f32[32,4,384]{2,1,0:T(4,128)} %pack.1), calls=%async_computation | async-start | bytes 393216 | tf_op jit(solution)/shard_map/all_to_all | solution.py:313
  31.5 0.7 copy-start.9
  31.5 0.8 copy-start.10
  48.8 0.7 copy-start
  51.2 8.9 %collective-permute-start.1 = (f32[328,128]{1,0:T(8,128)}, f32[328,128]{1,0:T(8,128)S(1)}, u32[]{:S(2)}, u32[]{:S(2)}) collective-permute-start(f32[328,128]{1,0:T(8,128)} %get-tuple-element.14.own_ref.h0_ref), channel_id=1, source_target_pairs={{1,0},{2,1},{3,2},{4,3},{5,4},{6,5},{7,6},{8,7},{9,8},{10,9},{11,1... | collective-permute-start | bytes 503816 | tf_op jit(solution)/shard_map/ppermute | solution.py:349
  55.8 5.6 %collective-permute-start = (f32[328,128]{1,0:T(8,128)}, f32[328,128]{1,0:T(8,128)S(1)}, u32[]{:S(2)}, u32[]{:S(2)}) collective-permute-start(f32[328,128]{1,0:T(8,128)} %get-tuple-element.14.own_ref.h0_ref), channel_id=1, source_target_pairs={{0,1},{1,2},{2,3},{3,4},{4,5},{5,6},{6,7},{7,8},{8,9},{9,10},{10,1... | collective-permute-start | bytes 503816 | tf_op jit(solution)/shard_map/ppermute | solution.py:348
  60.1 2.0 %copy-start.1 = (f32[328,128]{1,0:T(8,128)}, f32[328,128]{1,0:T(8,128)S(1)}, u32[]{:S(2)}) copy-start(f32[328,128]{1,0:T(8,128)S(1)} %collective-permute-done.1.right_ref) | copy-start | bytes 503812
  61.4 0.7 copy-start.2
  64.7 8.5 %collective-permute-start.3 = (f32[328,128]{1,0:T(8,128)}, f32[328,128]{1,0:T(8,128)S(1)}, u32[]{:S(2)}, u32[]{:S(2)}) collective-permute-start(f32[328,128]{1,0:T(8,128)} %get-tuple-element.18.own_ref), channel_id=1, source_target_pairs={{1,0},{2,1},{3,2},{4,3},{5,4},{6,5},{7,6},{8,7},{9,8},{10,9},{11,1... | collective-permute-start | bytes 503816 | tf_op jit(solution)/shard_map/ppermute | solution.py:349
  67.9 6.5 %collective-permute-start.2 = (f32[328,128]{1,0:T(8,128)}, f32[328,128]{1,0:T(8,128)S(1)}, u32[]{:S(2)}, u32[]{:S(2)}) collective-permute-start(f32[328,128]{1,0:T(8,128)} %get-tuple-element.18.own_ref), channel_id=1, source_target_pairs={{0,1},{1,2},{2,3},{3,4},{4,5},{5,6},{6,7},{7,8},{8,9},{9,10},{10,1... | collective-permute-start | bytes 503816 | tf_op jit(solution)/shard_map/ppermute | solution.py:348
  73.2 1.2 copy-start.3
  74.4 0.7 copy-start.5
  77.7 8.5 %collective-permute-start.5 = (f32[328,128]{1,0:T(8,128)}, f32[328,128]{1,0:T(8,128)S(1)}, u32[]{:S(2)}, u32[]{:S(2)}) collective-permute-start(f32[328,128]{1,0:T(8,128)} %get-tuple-element.20.own_ref), channel_id=1, source_target_pairs={{1,0},{2,1},{3,2},{4,3},{5,4},{6,5},{7,6},{8,7},{9,8},{10,9},{11,1... | collective-permute-start | bytes 503816 | tf_op jit(solution)/shard_map/ppermute | solution.py:349
  80.0 7.4 %collective-permute-start.4 = (f32[328,128]{1,0:T(8,128)}, f32[328,128]{1,0:T(8,128)S(1)}, u32[]{:S(2)}, u32[]{:S(2)}) collective-permute-start(f32[328,128]{1,0:T(8,128)} %get-tuple-element.20.own_ref), channel_id=1, source_target_pairs={{0,1},{1,2},{2,3},{3,4},{4,5},{5,6},{6,7},{7,8},{8,9},{9,10},{10,1... | collective-permute-start | bytes 503816 | tf_op jit(solution)/shard_map/ppermute | solution.py:348
  86.2 1.2 copy-start.4
  87.4 0.7 copy-start.6
  90.7 8.5 %collective-permute-start.7 = (f32[328,128]{1,0:T(8,128)}, f32[328,128]{1,0:T(8,128)S(1)}, u32[]{:S(2)}, u32[]{:S(2)}) collective-permute-start(f32[328,128]{1,0:T(8,128)} %get-tuple-element.22.own_ref), channel_id=1, source_target_pairs={{1,0},{2,1},{3,2},{4,3},{5,4},{6,5},{7,6},{8,7},{9,8},{10,9},{11,1... | collective-permute-start | bytes 503816 | tf_op jit(solution)/shard_map/ppermute | solution.py:349
  92.6 7.8 %collective-permute-start.6 = (f32[328,128]{1,0:T(8,128)}, f32[328,128]{1,0:T(8,128)S(1)}, u32[]{:S(2)}, u32[]{:S(2)}) collective-permute-start(f32[328,128]{1,0:T(8,128)} %get-tuple-element.22.own_ref), channel_id=1, source_target_pairs={{0,1},{1,2},{2,3},{3,4},{4,5},{5,6},{6,7},{7,8},{8,9},{9,10},{10,1... | collective-permute-start | bytes 503816 | tf_op jit(solution)/shard_map/ppermute | solution.py:348
  99.2 1.2 copy-start.7
  100.4 0.7 copy-start.8

commit v2 on v1

--- a/solution.py
+++ b/solution.py
@@ -70,7 +70,9 @@
     return tiles
 
 
-def prepare_kernel(mean_ref, wall_ref, position_ref, mean_out, wall_out, packed_out, rows_ref):
+def prepare_kernel(
+    mean_ref, wall_ref, position_ref, mean_out, wall_out, packed_out, speed_out, rows_ref
+):
     for cell in range(CELLS):
         for c1 in range(C1):
             cols = slice(c1 * LANES, (c1 + 1) * LANES)
@@ -87,6 +89,8 @@
             mean_out[start : start + 8, :] = picked
         else:
             wall_out[start - M_ROWS : start - M_ROWS + 8, :] = picked
+    momentum = rows_ref[m_row(1, 0) : m_row(2, 0), :]
+    speed_out[...] = jnp.full((8, LANES), jnp.sum(momentum * momentum), jnp.float32)
     packed_out[...] = pack_mean(
         [mean_out[i * C1 : (i + 1) * C1, :] for i in range(VARS * CELLS)]
     )
@@ -289,6 +293,23 @@
     return jax.ShapeDtypeStruct(shape, jnp.float32)
 
 
+def kept(*shape):
+    return pltpu.VMEM(shape, jnp.float32)
+
+
+def held(*arrays):
+    return [pltpu.with_memory_space_constraint(array, pltpu.VMEM) for array in arrays]
+
+
+def summed(value, axis):
+    count = lax.axis_size(axis)
+    reach = 1
+    while reach < count:
+        value = value + lax.ppermute(value, axis, [(i, i ^ reach) for i in range(count)])
+        reach *= 2
+    return value
+
+
 VMEM = pl.BlockSpec(memory_space=pltpu.VMEM)
 SMEM = pl.BlockSpec(memory_space=pltpu.SMEM)
 
@@ -304,30 +325,27 @@
 
     sends = pl.pallas_call(
         pack_kernel,
-        out_shape=f32(32, 4, 384),
+        out_shape=kept(32, 4, 384),
         in_specs=[VMEM, SMEM],
         out_specs=VMEM,
         scratch_shapes=rows_scratch(384, LANES),
         name="pack",
     )(harmonics, freq_index)
+    sends, mean_flow, wall_mask, jacobian_x, jacobian_y = lax.optimization_barrier(
+        (sends, mean_flow, wall_mask, jacobian_x, jacobian_y)
+    )
     arrived = lax.all_to_all(sends, "harm", 0, 0, tiled=True)
 
-    speed = jnp.sum(mean_flow[1] * mean_flow[1])
-    speeds = lax.all_to_all(
-        jnp.broadcast_to(speed, (slab_count, 1, LANES)), "slab", 0, 0, tiled=True
-    )
-    speed_total = jnp.sum(speeds, axis=0)
-    cell_count = CELLS * slab_count * plane_count
-    step = COURANT / (1.0 + jnp.sqrt(speed_total / cell_count))
-
-    mean_start, wall, packed = pl.pallas_call(
+    mean_start, wall, packed, speed = pl.pallas_call(
         prepare_kernel,
-        out_shape=(f32(M_ROWS, LANES), f32(W_ROWS, LANES), f32(8, LANES)),
+        out_shape=(kept(M_ROWS, LANES), kept(W_ROWS, LANES), kept(8, LANES), kept(8, LANES)),
         in_specs=[VMEM, VMEM, SMEM],
-        out_specs=(VMEM, VMEM, VMEM),
+        out_specs=(VMEM,) * 4,
         scratch_shapes=rows_scratch(M_ROWS + W_ROWS, LANES),
         name="prepare",
     )(mean_flow, wall_mask, position.astype(jnp.int32).reshape(1))
+    cell_count = CELLS * slab_count * plane_count
+    step = COURANT / (1.0 + jnp.sqrt(summed(speed, "slab") / cell_count))
     radial = 2 * position + jnp.arange(LANES) % 2
     radius = (HUB_RADIUS + (radial.astype(jnp.float32) + 0.5) / NZ).reshape(1, LANES)
     jac = jnp.concatenate([jacobian_x.reshape(-1, 1), jacobian_y.reshape(-1, 1)])
@@ -335,12 +353,12 @@
 
     state, omega = pl.pallas_call(
         unpack_kernel,
-        out_shape=(f32(H_ROWS + 8, LANES), f32(8, LANES)),
+        out_shape=(kept(H_ROWS + 8, LANES), kept(8, LANES)),
         in_specs=[VMEM, VMEM],
         out_specs=(VMEM, VMEM),
         scratch_shapes=rows_scratch(LANES, 384),
         name="unpack",
-    )(arrived, packed)
+    )(*held(arrived, packed))
 
     start, mean_now = state, mean_start
     for index, rate in enumerate(SECTION_RATES):
@@ -348,10 +366,10 @@
         left = lax.ppermute(state, "slab", [(i, i + 1) for i in range(slab_count - 1)])
         right = lax.ppermute(state, "slab", [(i + 1, i) for i in range(slab_count - 1)])
         if last:
-            shapes, scratch = f32(32, 4, 512), rows_scratch(512, LANES)
+            shapes, scratch = kept(32, 4, 512), rows_scratch(512, LANES)
             specs = VMEM
         else:
-            shapes, scratch = (f32(H_ROWS + 8, LANES), f32(M_ROWS, LANES)), []
+            shapes, scratch = (kept(H_ROWS + 8, LANES), kept(M_ROWS, LANES)), []
             specs = (VMEM, VMEM)
         result = pl.pallas_call(
             functools.partial(section_kernel, rate=rate, last=last),
@@ -360,7 +378,11 @@
             out_specs=specs,
             scratch_shapes=scratch,
             name=f"section{index}",
-        )(state, left, right, start, mean_start, mean_now, omega, wall, jac, step, radius)
+        )(
+            *held(
+                state, left, right, start, mean_start, mean_now, omega, wall, jac, step, radius
+            )
+        )
         if not last:
             state, mean_now = result
     back = lax.all_to_all(result, "harm", 0, 0, tiled=True)
@@ -371,7 +393,7 @@
         out_specs=(VMEM, VMEM),
         scratch_shapes=rows_scratch(LANES, 512),
         name="restore",
-    )(back)
+    )(*held(back))
 
 
 def solution(mesh):

time: 133 us -> 119 us (0.89)
  waiting for transfers between devices: 25.8 us -> 13.3 us
  Pallas kernels: 17.9 us -> 7.01 us
  blocking collectives: 26.4 us -> 36.1 us
  starting transfers between devices: 52.7 us -> 59.7 us
  local copies, waits for them, and re-layouts: 5.42 us -> 0.24 us
  other arithmetic: 2.57 us -> 0.11 us
    all_to_all x1, waiting for transfers between devices: 14.1 us -> 0.01 us  [shards(): arrived = lax.all_to_all(sends, 'harm', 0, 0, tiled=True)]
    ppermute x0 -> x4, starting transfers between devices: none -> 13.7 us  [summed(): lax.ppermute(value, axis, [(i, i ^ reach) for i in range(count)])]
    all_to_all x1, blocking collectives: 26.4 us -> 36.1 us  [shards(): back = lax.all_to_all(result, 'harm', 0, 0, tiled=True)]
    pallas_call x4, Pallas kernels: 10.8 us -> 3.13 us  [shards(): pl.pallas_call(functools.partial(section_kernel, rate=rate, last=last), o...]
    all_to_all x1 -> x0, starting transfers between devices: 6.23 us -> none  [shards(): lax.all_to_all(jnp.broadcast_to(speed, (slab_count, 1, LANES)), 'slab', 0...]
    ppermute x0 -> x4, waiting for transfers between devices: none -> 4.22 us  [summed(): lax.ppermute(value, axis, [(i, i ^ reach) for i in range(count)])]
    unnamed x22 -> x4, local copies, waits for them, and re-layouts: 3.33 us -> 0.01 us
    pallas_call x3, Pallas kernels: 5.21 us -> 2.98 us  [the longest x1 1.81 us: shards(): pl.pallas_call(pack_kernel, out_shape=kept(32, 4, 384), in_specs=[VMEM, S...]
  transfers between devices with their start and end apart: 10 -> 13, of which waited for: 10 -> 11; matrix products, arithmetic and copies ran while one was open for 1% -> 0% of each run, Pallas kernels for 3% -> 1%
where the time goes in v2:
time: 119 us; the launch traced here: 118 us
  starting transfers between devices  59.7 us (50%)
  blocking collectives  36.1 us (30%)
  waiting for transfers between devices  13.3 us (11%)
  Pallas kernels  7.01 us (6%)
  between operations  1.47 us (1%)
    all_to_all x1, blocking collectives, shards(): back = lax.all_to_all(result, 'harm', 0, 0, tiled=True)  36.1 us
    all_to_all x1, starting transfers between devices, shards(): arrived = lax.all_to_all(sends, 'harm', 0, 0, tiled=True)  17.6 us
    ppermute x4, starting transfers between devices, shards(): lax.ppermute(state, 'slab', [(i, i + 1) for i in range(slab_count - 1)])  15.3 us
    ppermute x4, starting transfers between devices, summed(): lax.ppermute(value, axis, [(i, i ^ reach) for i in range(count)])  13.7 us
    ppermute x4, starting transfers between devices, shards(): lax.ppermute(state, 'slab', [(i + 1, i) for i in range(slab_count - 1)])  13.1 us
    ppermute x4, waiting for transfers between devices, shards(): lax.ppermute(state, 'slab', [(i + 1, i) for i in range(slab_count - 1)])  4.57 us
    ppermute x4, waiting for transfers between devices, shards(): lax.ppermute(state, 'slab', [(i, i + 1) for i in range(slab_count - 1)])  4.54 us
    ppermute x4, waiting for transfers between devices, summed(): lax.ppermute(value, axis, [(i, i ^ reach) for i in range(count)])  4.22 us
  transfers between devices with their start and end apart: 13, of which 11 were waited for; matrix products, arithmetic and copies ran while one was open for 0% of the time, Pallas kernels for 1%

profile of v2, /device:TPU:7, one launch (start us, length us, event | category | flops | bytes accessed | tf_op | source)
XLA Modules:
  0.0 118.0 jit_solution(18185627909181170647)
XLA Ops:
  1.3 1.8 %pack.1 = f32[32,4,384]{2,1,0:T(4,128)} custom-call(f32[1,2,5,2,2048]{4,3,2,1,0:T(2,128)} %harm_ref.1, s32[1]{0:T(128)S(6)} %copy.8.freq_ref), custom_call_target="tpu_custom_call" | custom-call | tf_op jit(solution)/shard_map/pack/pallas_call | solution.py:326
  3.1 17.6 %all-to-all-start = ((f32[32,4,384]{2,1,0:T(4,128)}), f32[32,4,384]{2,1,0:T(4,128)S(1)}, u32[]{:S(2)}, u32[]{:S(2)}) async-start(f32[32,4,384]{2,1,0:T(4,128)} %pack.1), calls=%async_computation | async-start | bytes 393216 | tf_op jit(solution)/shard_map/all_to_all | solution.py:337
  20.7 1.0 prepare.1
  21.8 3.1 %collective-permute-start.2 = (f32[8,128]{1,0:T(8,128)S(1)}, f32[8,128]{1,0:T(8,128)S(1)}, u32[]{:S(2)}, u32[]{:S(2)}) collective-permute-start(f32[8,128]{1,0:T(8,128)S(1)} %get-tuple-element.29), channel_id=1, source_target_pairs={{0,1},{1,0},{2,3},{3,2},{4,5},{5,4},{6,7},{7,6},{8,9},{9,8},{10,11... | collective-permute-start | bytes 12296 | tf_op jit(solution)/shard_map/ppermute | solution.py:308
  24.9 0.8 collective-permute-done.2
  25.8 2.4 %collective-permute-start.3 = (f32[8,128]{1,0:T(8,128)S(1)}, f32[8,128]{1,0:T(8,128)S(1)}, u32[]{:S(2)}, u32[]{:S(2)}) collective-permute-start(f32[8,128]{1,0:T(8,128)S(1)} %add.64), channel_id=1, source_target_pairs={{0,2},{1,3},{2,0},{3,1},{4,6},{5,7},{6,4},{7,5},{8,10},{9,11},{10,... | collective-permute-start | bytes 12296 | tf_op jit(solution)/shard_map/ppermute | solution.py:308
  28.2 0.0 copy-start
  28.2 2.2 %collective-permute-done.3 = f32[8,128]{1,0:T(8,128)S(1)} collective-permute-done((f32[8,128]{1,0:T(8,128)S(1)}, f32[8,128]{1,0:T(8,128)S(1)}, u32[]{:S(2)}, u32[]{:S(2)}) %collective-permute-start.3) | collective-permute-done | bytes 4128 | tf_op jit(solution)/shard_map/ppermute | solution.py:308
  30.4 0.0 copy-start.1
  30.4 3.3 %collective-permute-start.4 = (f32[8,128]{1,0:T(8,128)S(1)}, f32[8,128]{1,0:T(8,128)S(1)}, u32[]{:S(2)}, u32[]{:S(2)}) collective-permute-start(f32[8,128]{1,0:T(8,128)S(1)} %add.65), channel_id=1, source_target_pairs={{0,4},{1,5},{2,6},{3,7},{4,0},{5,1},{6,2},{7,3},{8,12},{9,13},{10,... | collective-permute-start | bytes 12296 | tf_op jit(solution)/shard_map/ppermute | solution.py:308
  33.7 0.0 copy-done
  33.8 0.1 reshape.52
  33.8 0.0 copy-done.1
  33.8 0.1 reshape.53
  33.9 1.3 %collective-permute-done.4 = f32[8,128]{1,0:T(8,128)S(1)} collective-permute-done((f32[8,128]{1,0:T(8,128)S(1)}, f32[8,128]{1,0:T(8,128)S(1)}, u32[]{:S(2)}, u32[]{:S(2)}) %collective-permute-start.4) | collective-permute-done | bytes 4128 | tf_op jit(solution)/shard_map/ppermute | solution.py:308
  35.2 4.8 %collective-permute-start.5 = (f32[8,128]{1,0:T(8,128)S(1)}, f32[8,128]{1,0:T(8,128)S(1)}, u32[]{:S(2)}, u32[]{:S(2)}) collective-permute-start(f32[8,128]{1,0:T(8,128)S(1)} %add.66), channel_id=1, source_target_pairs={{0,8},{1,9},{2,10},{3,11},{4,12},{5,13},{6,14},{7,15},{8,0},{9,1},... | collective-permute-start | bytes 12296 | tf_op jit(solution)/shard_map/ppermute | solution.py:308
  40.0 0.1 maximum_bitcast_fusion
  40.1 0.0 all-to-all-done.arrived_ref
  40.1 0.1 unpack.1
  40.2 4.2 %collective-permute-start.1 = (f32[328,128]{1,0:T(8,128)S(1)}, f32[328,128]{1,0:T(8,128)S(1)}, u32[]{:S(2)}, u32[]{:S(2)}) collective-permute-start(f32[328,128]{1,0:T(8,128)S(1)} %get-tuple-element.23.own_ref.h0_ref), channel_id=1, source_target_pairs={{1,0},{2,1},{3,2},{4,3},{5,4},{6,5},{7,6},{8,7},{9,8},{10,9},{11,1... | collective-permute-start | bytes 503816 | tf_op jit(solution)/shard_map/ppermute | solution.py:367
  44.4 2.5 %collective-permute-start = (f32[328,128]{1,0:T(8,128)S(1)}, f32[328,128]{1,0:T(8,128)S(1)}, u32[]{:S(2)}, u32[]{:S(2)}) collective-permute-start(f32[328,128]{1,0:T(8,128)S(1)} %get-tuple-element.23.own_ref.h0_ref), channel_id=1, source_target_pairs={{0,1},{1,2},{2,3},{3,4},{4,5},{5,6},{6,7},{7,8},{8,9},{9,10},{10,1... | collective-permute-start | bytes 503816 | tf_op jit(solution)/shard_map/ppermute | solution.py:366
  46.9 0.0 collective-permute-done.5
  46.9 1.1 collective-permute-done.1.right_ref
  48.0 1.2 %collective-permute-done.left_ref = f32[328,128]{1,0:T(8,128)S(1)} collective-permute-done((f32[328,128]{1,0:T(8,128)S(1)}, f32[328,128]{1,0:T(8,128)S(1)}, u32[]{:S(2)}, u32[]{:S(2)}) %collective-permute-start) | collective-permute-done | bytes 167968 | tf_op jit(solution)/shard_map/ppermute | solution.py:366
  49.2 0.1 broadcast_in_dim.8.jac_ref
  49.3 0.7 section0.1
  50.0 3.8 %collective-permute-start.7 = (f32[328,128]{1,0:T(8,128)S(1)}, f32[328,128]{1,0:T(8,128)S(1)}, u32[]{:S(2)}, u32[]{:S(2)}) collective-permute-start(f32[328,128]{1,0:T(8,128)S(1)} %get-tuple-element.30.own_ref), channel_id=1, source_target_pairs={{1,0},{2,1},{3,2},{4,3},{5,4},{6,5},{7,6},{8,7},{9,8},{10,9},{11,1... | collective-permute-start | bytes 503816 | tf_op jit(solution)/shard_map/ppermute | solution.py:367
  53.9 3.4 %collective-permute-start.6 = (f32[328,128]{1,0:T(8,128)S(1)}, f32[328,128]{1,0:T(8,128)S(1)}, u32[]{:S(2)}, u32[]{:S(2)}) collective-permute-start(f32[328,128]{1,0:T(8,128)S(1)} %get-tuple-element.30.own_ref), channel_id=1, source_target_pairs={{0,1},{1,2},{2,3},{3,4},{4,5},{5,6},{6,7},{7,8},{8,9},{9,10},{10,1... | collective-permute-start | bytes 503816 | tf_op jit(solution)/shard_map/ppermute | solution.py:366
  57.2 1.2 collective-permute-done.7.right_ref
  58.4 1.1 collective-permute-done.6.left_ref
  59.5 0.7 section1.1
  60.2 2.9 %collective-permute-start.9 = (f32[328,128]{1,0:T(8,128)S(1)}, f32[328,128]{1,0:T(8,128)S(1)}, u32[]{:S(2)}, u32[]{:S(2)}) collective-permute-start(f32[328,128]{1,0:T(8,128)S(1)} %get-tuple-element.32.own_ref), channel_id=1, source_target_pairs={{1,0},{2,1},{3,2},{4,3},{5,4},{6,5},{7,6},{8,7},{9,8},{10,9},{11,1... | collective-permute-start | bytes 503816 | tf_op jit(solution)/shard_map/ppermute | solution.py:367
  63.2 4.3 %collective-permute-start.8 = (f32[328,128]{1,0:T(8,128)S(1)}, f32[328,128]{1,0:T(8,128)S(1)}, u32[]{:S(2)}, u32[]{:S(2)}) collective-permute-start(f32[328,128]{1,0:T(8,128)S(1)} %get-tuple-element.32.own_ref), channel_id=1, source_target_pairs={{0,1},{1,2},{2,3},{3,4},{4,5},{5,6},{6,7},{7,8},{8,9},{9,10},{10,1... | collective-permute-start | bytes 503816 | tf_op jit(solution)/shard_map/ppermute | solution.py:366
  67.5 1.2 collective-permute-done.9.right_ref
  68.6 1.1 collective-permute-done.8.left_ref
  69.7 0.7 section2.1
  70.5 2.0 %collective-permute-start.11 = (f32[328,128]{1,0:T(8,128)S(1)}, f32[328,128]{1,0:T(8,128)S(1)}, u32[]{:S(2)}, u32[]{:S(2)}) collective-permute-start(f32[328,128]{1,0:T(8,128)S(1)} %get-tuple-element.34.own_ref), channel_id=1, source_target_pairs={{1,0},{2,1},{3,2},{4,3},{5,4},{6,5},{7,6},{8,7},{9,8},{10,9},{11,1... | collective-permute-start | bytes 503816 | tf_op jit(solution)/shard_map/ppermute | solution.py:367
  72.5 5.2 %collective-permute-start.10 = (f32[328,128]{1,0:T(8,128)S(1)}, f32[328,128]{1,0:T(8,128)S(1)}, u32[]{:S(2)}, u32[]{:S(2)}) collective-permute-start(f32[328,128]{1,0:T(8,128)S(1)} %get-tuple-element.34.own_ref), channel_id=1, source_target_pairs={{0,1},{1,2},{2,3},{3,4},{4,5},{5,6},{6,7},{7,8},{8,9},{9,10},{10,1... | collective-permute-start | bytes 503816 | tf_op jit(solution)/shard_map/ppermute | solution.py:366
  77.7 1.2 collective-permute-done.11.right_ref
  78.9 1.1 collective-permute-done.10.left_ref
  80.0 1.0 section3.1
  81.0 36.1 %all_to_all.10.arrived_ref = f32[32,4,512]{2,1,0:T(4,128)S(1)} all-to-all(f32[32,4,512]{2,1,0:T(4,128)S(1)} %section3.1), channel_id=1, replica_groups=mesh['harm'=32,'slab'=16] {'harm'}, dimensions={0} | all-to-all | bytes 524288 | tf_op jit(solution)/shard_map/all_to_all | solution.py:388
  117.1 0.9 restore.1
  (5 shorter events, 0.0 us)
Async XLA Ops:
  3.1 37.0 %all-to-all-start = ((f32[32,4,384]{2,1,0:T(4,128)}), f32[32,4,384]{2,1,0:T(4,128)S(1)}, u32[]{:S(2)}, u32[]{:S(2)}) async-start(f32[32,4,384]{2,1,0:T(4,128)} %pack.1), calls=%async_computation | async-start | bytes 393216 | tf_op jit(solution)/shard_map/all_to_all | solution.py:337
  21.8 4.0 %collective-permute-start.2 = (f32[8,128]{1,0:T(8,128)S(1)}, f32[8,128]{1,0:T(8,128)S(1)}, u32[]{:S(2)}, u32[]{:S(2)}) collective-permute-start(f32[8,128]{1,0:T(8,128)S(1)} %get-tuple-element.29), channel_id=1, source_target_pairs={{0,1},{1,0},{2,3},{3,2},{4,5},{5,4},{6,7},{7,6},{8,9},{9,8},{10,11... | collective-permute-start | bytes 12296 | tf_op jit(solution)/shard_map/ppermute | solution.py:308
  25.8 4.6 %collective-permute-start.3 = (f32[8,128]{1,0:T(8,128)S(1)}, f32[8,128]{1,0:T(8,128)S(1)}, u32[]{:S(2)}, u32[]{:S(2)}) collective-permute-start(f32[8,128]{1,0:T(8,128)S(1)} %add.64), channel_id=1, source_target_pairs={{0,2},{1,3},{2,0},{3,1},{4,6},{5,7},{6,4},{7,5},{8,10},{9,11},{10,... | collective-permute-start | bytes 12296 | tf_op jit(solution)/shard_map/ppermute | solution.py:308
  28.2 5.5 %copy-start = (f32[5,5]{1,0:T(8,128)S(1)}, f32[5,5]{1,0:T(8,128)}, u32[]{:S(2)}) copy-start(f32[5,5]{1,0:T(8,128)} %param.10) | copy-start | bytes 304
  30.4 3.4 %copy-start.1 = (f32[5,5]{1,0:T(8,128)S(1)}, f32[5,5]{1,0:T(8,128)}, u32[]{:S(2)}) copy-start(f32[5,5]{1,0:T(8,128)} %param.11) | copy-start | bytes 304
  30.4 4.8 %collective-permute-start.4 = (f32[8,128]{1,0:T(8,128)S(1)}, f32[8,128]{1,0:T(8,128)S(1)}, u32[]{:S(2)}, u32[]{:S(2)}) collective-permute-start(f32[8,128]{1,0:T(8,128)S(1)} %add.65), channel_id=1, source_target_pairs={{0,4},{1,5},{2,6},{3,7},{4,0},{5,1},{6,2},{7,3},{8,12},{9,13},{10,... | collective-permute-start | bytes 12296 | tf_op jit(solution)/shard_map/ppermute | solution.py:308
  35.2 11.8 %collective-permute-start.5 = (f32[8,128]{1,0:T(8,128)S(1)}, f32[8,128]{1,0:T(8,128)S(1)}, u32[]{:S(2)}, u32[]{:S(2)}) collective-permute-start(f32[8,128]{1,0:T(8,128)S(1)} %add.66), channel_id=1, source_target_pairs={{0,8},{1,9},{2,10},{3,11},{4,12},{5,13},{6,14},{7,15},{8,0},{9,1},... | collective-permute-start | bytes 12296 | tf_op jit(solution)/shard_map/ppermute | solution.py:308
  40.2 7.8 %collective-permute-start.1 = (f32[328,128]{1,0:T(8,128)S(1)}, f32[328,128]{1,0:T(8,128)S(1)}, u32[]{:S(2)}, u32[]{:S(2)}) collective-permute-start(f32[328,128]{1,0:T(8,128)S(1)} %get-tuple-element.23.own_ref.h0_ref), channel_id=1, source_target_pairs={{1,0},{2,1},{3,2},{4,3},{5,4},{6,5},{7,6},{8,7},{9,8},{10,9},{11,1... | collective-permute-start | bytes 503816 | tf_op jit(solution)/shard_map/ppermute | solution.py:367
  44.4 4.8 %collective-permute-start = (f32[328,128]{1,0:T(8,128)S(1)}, f32[328,128]{1,0:T(8,128)S(1)}, u32[]{:S(2)}, u32[]{:S(2)}) collective-permute-start(f32[328,128]{1,0:T(8,128)S(1)} %get-tuple-element.23.own_ref.h0_ref), channel_id=1, source_target_pairs={{0,1},{1,2},{2,3},{3,4},{4,5},{5,6},{6,7},{7,8},{8,9},{9,10},{10,1... | collective-permute-start | bytes 503816 | tf_op jit(solution)/shard_map/ppermute | solution.py:366
  50.0 8.4 %collective-permute-start.7 = (f32[328,128]{1,0:T(8,128)S(1)}, f32[328,128]{1,0:T(8,128)S(1)}, u32[]{:S(2)}, u32[]{:S(2)}) collective-permute-start(f32[328,128]{1,0:T(8,128)S(1)} %get-tuple-element.30.own_ref), channel_id=1, source_target_pairs={{1,0},{2,1},{3,2},{4,3},{5,4},{6,5},{7,6},{8,7},{9,8},{10,9},{11,1... | collective-permute-start | bytes 503816 | tf_op jit(solution)/shard_map/ppermute | solution.py:367
  53.9 5.7 %collective-permute-start.6 = (f32[328,128]{1,0:T(8,128)S(1)}, f32[328,128]{1,0:T(8,128)S(1)}, u32[]{:S(2)}, u32[]{:S(2)}) collective-permute-start(f32[328,128]{1,0:T(8,128)S(1)} %get-tuple-element.30.own_ref), channel_id=1, source_target_pairs={{0,1},{1,2},{2,3},{3,4},{4,5},{5,6},{6,7},{7,8},{8,9},{9,10},{10,1... | collective-permute-start | bytes 503816 | tf_op jit(solution)/shard_map/ppermute | solution.py:366
  60.2 8.4 %collective-permute-start.9 = (f32[328,128]{1,0:T(8,128)S(1)}, f32[328,128]{1,0:T(8,128)S(1)}, u32[]{:S(2)}, u32[]{:S(2)}) collective-permute-start(f32[328,128]{1,0:T(8,128)S(1)} %get-tuple-element.32.own_ref), channel_id=1, source_target_pairs={{1,0},{2,1},{3,2},{4,3},{5,4},{6,5},{7,6},{8,7},{9,8},{10,9},{11,1... | collective-permute-start | bytes 503816 | tf_op jit(solution)/shard_map/ppermute | solution.py:367
  63.2 6.6 %collective-permute-start.8 = (f32[328,128]{1,0:T(8,128)S(1)}, f32[328,128]{1,0:T(8,128)S(1)}, u32[]{:S(2)}, u32[]{:S(2)}) collective-permute-start(f32[328,128]{1,0:T(8,128)S(1)} %get-tuple-element.32.own_ref), channel_id=1, source_target_pairs={{0,1},{1,2},{2,3},{3,4},{4,5},{5,6},{6,7},{7,8},{8,9},{9,10},{10,1... | collective-permute-start | bytes 503816 | tf_op jit(solution)/shard_map/ppermute | solution.py:366
  70.5 8.4 %collective-permute-start.11 = (f32[328,128]{1,0:T(8,128)S(1)}, f32[328,128]{1,0:T(8,128)S(1)}, u32[]{:S(2)}, u32[]{:S(2)}) collective-permute-start(f32[328,128]{1,0:T(8,128)S(1)} %get-tuple-element.34.own_ref), channel_id=1, source_target_pairs={{1,0},{2,1},{3,2},{4,3},{5,4},{6,5},{7,6},{8,7},{9,8},{10,9},{11,1... | collective-permute-start | bytes 503816 | tf_op jit(solution)/shard_map/ppermute | solution.py:367
  72.5 7.5 %collective-permute-start.10 = (f32[328,128]{1,0:T(8,128)S(1)}, f32[328,128]{1,0:T(8,128)S(1)}, u32[]{:S(2)}, u32[]{:S(2)}) collective-permute-start(f32[328,128]{1,0:T(8,128)S(1)} %get-tuple-element.34.own_ref), channel_id=1, source_target_pairs={{0,1},{1,2},{2,3},{3,4},{4,5},{5,6},{6,7},{7,8},{8,9},{9,10},{10,1... | collective-permute-start | bytes 503816 | tf_op jit(solution)/shard_map/ppermute | solution.py:366

commit v3 on v2

--- a/solution.py
+++ b/solution.py
@@ -6,6 +6,7 @@
 from jax.experimental import pallas as pl
 from jax.experimental.pallas import tpu as pltpu
 from jax.sharding import PartitionSpec as P
+
 
 NZ = 64
 EPS_FOURTH = 0.05
@@ -33,7 +34,7 @@
     return (var * CELLS + cell) * C1
 
 
-def pack_kernel(harm_ref, freq_ref, out_ref, rows_ref):
+def pack_kernel(harm_ref, freq_ref, out_ref, token_ref, rows_ref):
     for part in range(2):
         for var in range(VARS):
             for cell in range(CELLS):
@@ -44,6 +45,7 @@
                     ]
     omega = OMEGA_BASE * freq_ref[0].astype(jnp.float32)
     rows_ref[H_ROWS:, :] = jnp.full((rows_ref.shape[0] - H_ROWS, LANES), omega, jnp.float32)
+    token_ref[...] = jnp.full((8, LANES), omega, jnp.float32)
     turned = rows_ref[...].T
     for j in range(32):
         out_ref[j, 0:2, :] = turned[2 * j : 2 * j + 2, :]
@@ -71,8 +73,9 @@
 
 
 def prepare_kernel(
-    mean_ref, wall_ref, position_ref, mean_out, wall_out, packed_out, speed_out, rows_ref
+    mean_ref, wall_ref, position_ref, token_ref, mean_out, wall_out, packed_out, speed_out, rows_ref
 ):
+    del token_ref
     for cell in range(CELLS):
         for c1 in range(C1):
             cols = slice(c1 * LANES, (c1 + 1) * LANES)
@@ -90,13 +93,14 @@
         else:
             wall_out[start - M_ROWS : start - M_ROWS + 8, :] = picked
     momentum = rows_ref[m_row(1, 0) : m_row(2, 0), :]
-    speed_out[...] = jnp.full((8, LANES), jnp.sum(momentum * momentum), jnp.float32)
+    speed_out[...] = jnp.full(speed_out.shape, jnp.sum(momentum * momentum), jnp.float32)
     packed_out[...] = pack_mean(
         [mean_out[i * C1 : (i + 1) * C1, :] for i in range(VARS * CELLS)]
     )
 
 
-def unpack_kernel(arrived_ref, packed_ref, state_out, omega_out, rows_ref):
+def unpack_kernel(arrived_ref, packed_ref, speed_ref, state_out, omega_out, speed_out, rows_ref):
+    speed_out[...] = speed_ref[...]
     for k in range(32):
         rows_ref[4 * k : 4 * k + 4, :] = arrived_ref[k]
     turned = rows_ref[...].T
@@ -105,10 +109,17 @@
     omega_out[...] = turned[H_ROWS : H_ROWS + 8, :]
 
 
-def section_kernel(
-    own_ref, left_ref, right_ref, h0_ref, m0_ref, mean_ref, omega_ref, wall_ref, jac_ref,
-    step_ref, radius_ref, *outs, rate, last
-):
+def section_kernel(*refs, stage, cell_count):
+    last = stage == len(SECTION_RATES) - 1
+    own_ref, left_ref, right_ref, mean_ref, omega_ref, wall_ref, jac_ref, radius_ref = refs[:8]
+    refs = refs[8:]
+    if stage == 0:
+        outs = refs
+    elif stage == 1:
+        speed_ref, own_res, left_res, right_res, mean_res, *outs = refs
+        h0_ref, m0_ref = own_ref, mean_ref
+    else:
+        speed_ref, h0_ref, m0_ref, *outs = refs
     lane = lax.broadcasted_iota(jnp.int32, (C1, LANES), 1)
     even = (lane // 2) % 2 == 0
 
@@ -134,26 +145,38 @@
             out.append(total)
         return out
 
+    omega = splat(omega_ref, 0)
+    if stage:
+        speed_total = jnp.sum(speed_ref[...], axis=0)
+        time_step = COURANT / (1.0 + jnp.sqrt(speed_total / cell_count))
+        time_step = jnp.broadcast_to(time_step, (C1, LANES))
+        step = SECTION_RATES[stage] * time_step
+    blocks = [(left_ref, None), (own_ref, None), (right_ref, None)]
+    mean_block = (mean_ref, None)
+    if stage == 1:
+        first = SECTION_RATES[0] * time_step
+        blocks = [(left_ref, left_res), (own_ref, own_res), (right_ref, right_res)]
+        mean_block = (mean_ref, mean_res)
+
+    def load(block, row, count=C1):
+        base, residual = block
+        value = base[row : row + count, :]
+        if residual is not None:
+            value = value + first[:count] * residual[row : row + count, :]
+        return value
+
     def column(part, var):
         row = h_row(part, var, 0)
-        return [
-            ref[row + C1 * cell : row + C1 * (cell + 1), :]
-            for ref in (left_ref, own_ref, right_ref)
-            for cell in range(CELLS)
-        ]
-
-    omega = splat(omega_ref, 0)
-    step = rate * splat(step_ref, 0)
+        return [load(block, row + C1 * cell) for block in blocks for cell in range(CELLS)]
+
     inv_radius = 1.0 / splat(radius_ref, 0)
 
     harm = [[column(part, var) for var in range(VARS)] for part in range(2)]
-    left_mean = unpack_mean(left_ref[H_ROWS:, :])
-    right_mean = unpack_mean(right_ref[H_ROWS:, :])
+    left_mean = unpack_mean(load(blocks[0], H_ROWS, 8))
+    right_mean = unpack_mean(load(blocks[2], H_ROWS, 8))
     mean = []
     for var in range(VARS):
-        own_mean = [
-            mean_ref[m_row(var, cell) : m_row(var, cell) + C1, :] for cell in range(CELLS)
-        ]
+        own_mean = [load(mean_block, m_row(var, cell)) for cell in range(CELLS)]
         mean.append(
             left_mean[CELLS * var : CELLS * (var + 1)]
             + own_mean
@@ -200,7 +223,9 @@
                     - wall * harm[part][var][at]
                 )
                 row = h_row(part, var, cell)
-                harm_new[part, var, cell] = h0_ref[row : row + C1, :] + step * res
+                if stage:
+                    res = h0_ref[row : row + C1, :] + step * res
+                harm_new[part, var, cell] = res
 
     def stress(index, at):
         a, b = STRESS_PAIRS[index]
@@ -244,7 +269,9 @@
             if var:
                 res = res + terms[var]
             row = m_row(var, cell)
-            mean_new[var, cell] = m0_ref[row : row + C1, :] + step * res
+            if stage:
+                res = m0_ref[row : row + C1, :] + step * res
+            mean_new[var, cell] = res
 
     if last:
         out_ref, rows_ref = outs
@@ -301,15 +328,6 @@
     return [pltpu.with_memory_space_constraint(array, pltpu.VMEM) for array in arrays]
 
 
-def summed(value, axis):
-    count = lax.axis_size(axis)
-    reach = 1
-    while reach < count:
-        value = value + lax.ppermute(value, axis, [(i, i ^ reach) for i in range(count)])
-        reach *= 2
-    return value
-
-
 VMEM = pl.BlockSpec(memory_space=pltpu.VMEM)
 SMEM = pl.BlockSpec(memory_space=pltpu.SMEM)
 
@@ -323,68 +341,77 @@
     slab_count = lax.axis_size("slab")
     position = lax.axis_index("harm")
 
-    sends = pl.pallas_call(
+    sends, token = pl.pallas_call(
         pack_kernel,
-        out_shape=kept(32, 4, 384),
+        out_shape=(kept(32, 4, 384), kept(8, LANES)),
         in_specs=[VMEM, SMEM],
-        out_specs=VMEM,
+        out_specs=(VMEM, VMEM),
         scratch_shapes=rows_scratch(384, LANES),
         name="pack",
     )(harmonics, freq_index)
-    sends, mean_flow, wall_mask, jacobian_x, jacobian_y = lax.optimization_barrier(
-        (sends, mean_flow, wall_mask, jacobian_x, jacobian_y)
-    )
     arrived = lax.all_to_all(sends, "harm", 0, 0, tiled=True)
 
     mean_start, wall, packed, speed = pl.pallas_call(
         prepare_kernel,
-        out_shape=(kept(M_ROWS, LANES), kept(W_ROWS, LANES), kept(8, LANES), kept(8, LANES)),
-        in_specs=[VMEM, VMEM, SMEM],
+        out_shape=(
+            kept(M_ROWS, LANES),
+            kept(W_ROWS, LANES),
+            kept(8, LANES),
+            kept(slab_count, 1, LANES),
+        ),
+        in_specs=[VMEM, VMEM, SMEM, VMEM],
         out_specs=(VMEM,) * 4,
         scratch_shapes=rows_scratch(M_ROWS + W_ROWS, LANES),
         name="prepare",
-    )(mean_flow, wall_mask, position.astype(jnp.int32).reshape(1))
-    cell_count = CELLS * slab_count * plane_count
-    step = COURANT / (1.0 + jnp.sqrt(summed(speed, "slab") / cell_count))
+    )(mean_flow, wall_mask, position.astype(jnp.int32).reshape(1), *held(token))
+    mean_start, jacobian_x, jacobian_y = lax.optimization_barrier(
+        (mean_start, jacobian_x, jacobian_y)
+    )
     radial = 2 * position + jnp.arange(LANES) % 2
     radius = (HUB_RADIUS + (radial.astype(jnp.float32) + 0.5) / NZ).reshape(1, LANES)
     jac = jnp.concatenate([jacobian_x.reshape(-1, 1), jacobian_y.reshape(-1, 1)])
     jac = jnp.broadcast_to(jac, (2 * VARS * VARS, LANES))
 
-    state, omega = pl.pallas_call(
+    start, omega, speed = pl.pallas_call(
         unpack_kernel,
-        out_shape=(kept(H_ROWS + 8, LANES), kept(8, LANES)),
-        in_specs=[VMEM, VMEM],
-        out_specs=(VMEM, VMEM),
+        out_shape=(kept(H_ROWS + 8, LANES), kept(8, LANES), kept(slab_count, 1, LANES)),
+        in_specs=[VMEM] * 3,
+        out_specs=(VMEM,) * 3,
         scratch_shapes=rows_scratch(LANES, 384),
         name="unpack",
-    )(*held(arrived, packed))
-
-    start, mean_now = state, mean_start
-    for index, rate in enumerate(SECTION_RATES):
-        last = index == len(SECTION_RATES) - 1
+    )(*held(arrived, packed, speed))
+
+    speeds = lax.all_to_all(speed, "slab", 0, 0, tiled=True)
+    cell_count = CELLS * slab_count * plane_count
+
+    def beside(state):
         left = lax.ppermute(state, "slab", [(i, i + 1) for i in range(slab_count - 1)])
         right = lax.ppermute(state, "slab", [(i + 1, i) for i in range(slab_count - 1)])
-        if last:
+        return state, left, right
+
+    def section(stage, *operands):
+        if stage == len(SECTION_RATES) - 1:
             shapes, scratch = kept(32, 4, 512), rows_scratch(512, LANES)
             specs = VMEM
         else:
             shapes, scratch = (kept(H_ROWS + 8, LANES), kept(M_ROWS, LANES)), []
             specs = (VMEM, VMEM)
-        result = pl.pallas_call(
-            functools.partial(section_kernel, rate=rate, last=last),
+        return pl.pallas_call(
+            functools.partial(section_kernel, stage=stage, cell_count=cell_count),
             out_shape=shapes,
-            in_specs=[VMEM] * 11,
+            in_specs=[VMEM] * len(operands),
             out_specs=specs,
             scratch_shapes=scratch,
-            name=f"section{index}",
-        )(
-            *held(
-                state, left, right, start, mean_start, mean_now, omega, wall, jac, step, radius
-            )
-        )
-        if not last:
-            state, mean_now = result
+        )(*held(*operands))
+
+    fixed = (omega, wall, jac, radius)
+    start_blocks = beside(start)
+    residual, mean_residual = section(0, *start_blocks, mean_start, *fixed)
+    state, mean_now = section(
+        1, *start_blocks, mean_start, *fixed, speeds, *beside(residual), mean_residual
+    )
+    state, mean_now = section(2, *beside(state), mean_now, *fixed, speeds, start, mean_start)
+    result = section(3, *beside(state), mean_now, *fixed, speeds, start, mean_start)
     back = lax.all_to_all(result, "harm", 0, 0, tiled=True)
     return pl.pallas_call(
         restore_kernel,

time: 119 us -> 115 us (0.966)
  the two profiles are of different devices: /device:TPU:7 before, /device:TPU:6 now
where the time goes in v3:
time: 115 us
  blocking collectives  39.3 us (34%)
  starting transfers between devices  36 us (31%)
  waiting for transfers between devices  30.7 us (27%)
  Pallas kernels  7.04 us (6%)
  between operations  1.42 us (1%)
    all_to_all x1, blocking collectives, shards(): back = lax.all_to_all(result, 'harm', 0, 0, tiled=True)  27.2 us
    all_to_all x1, starting transfers between devices, shards(): arrived = lax.all_to_all(sends, 'harm', 0, 0, tiled=True)  18.2 us
    all_to_all x1, waiting for transfers between devices, shards(): arrived = lax.all_to_all(sends, 'harm', 0, 0, tiled=True)  17.7 us
    all_to_all x1, blocking collectives, shards(): speeds = lax.all_to_all(speed, 'slab', 0, 0, tiled=True)  12.1 us
    ppermute x4, waiting for transfers between devices, beside(): lax.ppermute(state, 'slab', [(i, i + 1) for i in range(slab_count - 1)])  11.5 us
    ppermute x4, starting transfers between devices, beside(): lax.ppermute(state, 'slab', [(i, i + 1) for i in range(slab_count - 1)])  9.14 us
    ppermute x4, starting transfers between devices, beside(): lax.ppermute(state, 'slab', [(i + 1, i) for i in range(slab_count - 1)])  8.7 us
    pallas_call x4, Pallas kernels, section(): pl.pallas_call(functools.partial(section_kernel, stage=stage, cell_count=...  3.16 us
  transfers between devices with their start and end apart: 9, of which 7 were waited for; matrix products, arithmetic and copies ran while one was open for 0% of the time, Pallas kernels for 1%

profile of v3, /device:TPU:6, one launch (start us, length us, event | category | flops | bytes accessed | tf_op | source)
XLA Modules:
  0.0 114.9 jit_solution(15358412003618741840)
XLA Ops:
  1.3 1.8 %pack.1 = (f32[32,4,384]{2,1,0:T(4,128)}, f32[8,128]{1,0:T(8,128)S(1)}) custom-call(f32[1,2,5,2,2048]{4,3,2,1,0:T(2,128)} %harm_ref.1, s32[1]{0:T(128)S(6)} %copy.8.freq_ref), custom_call_target="tpu_custom_call" | custom-call | tf_op jit(solution)/shard_map/pack/pallas_call | solution.py:344
  3.1 18.2 %all-to-all-start = ((f32[32,4,384]{2,1,0:T(4,128)}), f32[32,4,384]{2,1,0:T(4,128)S(1)}, u32[]{:S(2)}, u32[]{:S(2)}) async-start(f32[32,4,384]{2,1,0:T(4,128)} %get-tuple-element.20), calls=%async_computation | async-start | bytes 393216 | tf_op jit(solution)/shard_map/all_to_all | solution.py:352
  21.3 1.0 prepare.1
  22.4 17.7 %all-to-all-done.arrived_ref = f32[32,4,384]{2,1,0:T(4,128)S(1)} async-done(((f32[32,4,384]{2,1,0:T(4,128)}), f32[32,4,384]{2,1,0:T(4,128)S(1)}, u32[]{:S(2)}, u32[]{:S(2)}) %all-to-all-start) | async-done | bytes 196640 | tf_op jit(solution)/shard_map/all_to_all | solution.py:352
  40.1 0.1 unpack.1
  40.2 0.0 copy-start
  40.2 0.0 copy-start.1
  40.2 2.1 %collective-permute-start.1 = (f32[328,128]{1,0:T(8,128)S(1)}, f32[328,128]{1,0:T(8,128)S(1)}, u32[]{:S(2)}, u32[]{:S(2)}) collective-permute-start(f32[328,128]{1,0:T(8,128)S(1)} %get-tuple-element.24.refs_0_.refs_9_), channel_id=1, source_target_pairs={{1,0},{2,1},{3,2},{4,3},{5,4},{6,5},{7,6},{8,7},{9,8},{10,9},{11,1... | collective-permute-start | bytes 503816 | tf_op jit(solution)/shard_map/ppermute | solution.py:389
  42.3 2.4 %collective-permute-start = (f32[328,128]{1,0:T(8,128)S(1)}, f32[328,128]{1,0:T(8,128)S(1)}, u32[]{:S(2)}, u32[]{:S(2)}) collective-permute-start(f32[328,128]{1,0:T(8,128)S(1)} %get-tuple-element.24.refs_0_.refs_9_), channel_id=1, source_target_pairs={{0,1},{1,2},{2,3},{3,4},{4,5},{5,6},{6,7},{7,8},{8,9},{9,10},{10,1... | collective-permute-start | bytes 503816 | tf_op jit(solution)/shard_map/ppermute | solution.py:388
  44.7 0.0 copy-done
  44.7 0.1 reshape.52
  44.8 0.0 copy-done.1
  44.8 0.1 reshape.53
  44.9 0.1 maximum_bitcast_fusion
  45.0 0.2 collective-permute-done.1.refs_2_
  45.1 3.8 %collective-permute-done.refs_1_ = f32[328,128]{1,0:T(8,128)S(1)} collective-permute-done((f32[328,128]{1,0:T(8,128)S(1)}, f32[328,128]{1,0:T(8,128)S(1)}, u32[]{:S(2)}, u32[]{:S(2)}) %collective-permute-start) | collective-permute-done | bytes 167968 | tf_op jit(solution)/shard_map/ppermute | solution.py:388
  49.0 0.1 broadcast_in_dim.8.refs_6_
  49.0 0.7 shard_map.77
  49.8 1.9 %collective-permute-start.3 = (f32[328,128]{1,0:T(8,128)S(1)}, f32[328,128]{1,0:T(8,128)S(1)}, u32[]{:S(2)}, u32[]{:S(2)}) collective-permute-start(f32[328,128]{1,0:T(8,128)S(1)} %get-tuple-element.32.refs_9_), channel_id=1, source_target_pairs={{1,0},{2,1},{3,2},{4,3},{5,4},{6,5},{7,6},{8,7},{9,8},{10,9},{11,1... | collective-permute-start | bytes 503816 | tf_op jit(solution)/shard_map/ppermute | solution.py:389
  51.7 2.4 %collective-permute-start.2 = (f32[328,128]{1,0:T(8,128)S(1)}, f32[328,128]{1,0:T(8,128)S(1)}, u32[]{:S(2)}, u32[]{:S(2)}) collective-permute-start(f32[328,128]{1,0:T(8,128)S(1)} %get-tuple-element.32.refs_9_), channel_id=1, source_target_pairs={{0,1},{1,2},{2,3},{3,4},{4,5},{5,6},{6,7},{7,8},{8,9},{9,10},{10,1... | collective-permute-start | bytes 503816 | tf_op jit(solution)/shard_map/ppermute | solution.py:388
  54.1 12.1 %all_to_all.15.refs_8_ = f32[16,1,128]{2,1,0:T(1,128)S(1)} all-to-all(f32[16,1,128]{2,1,0:T(1,128)S(1)} %get-tuple-element.31), channel_id=1, replica_groups=mesh['harm'=32,'slab'=16] {'slab'}, dimensions={0} | all-to-all | bytes 16384 | tf_op jit(solution)/shard_map/all_to_all | solution.py:384
  66.2 0.0 collective-permute-done.3.refs_11_
  66.2 0.0 collective-permute-done.2.refs_10_
  66.2 0.7 shard_map.78
  67.0 2.8 %collective-permute-start.5 = (f32[328,128]{1,0:T(8,128)S(1)}, f32[328,128]{1,0:T(8,128)S(1)}, u32[]{:S(2)}, u32[]{:S(2)}) collective-permute-start(f32[328,128]{1,0:T(8,128)S(1)} %get-tuple-element.34.refs_0_), channel_id=1, source_target_pairs={{1,0},{2,1},{3,2},{4,3},{5,4},{6,5},{7,6},{8,7},{9,8},{10,9},{11,1... | collective-permute-start | bytes 503816 | tf_op jit(solution)/shard_map/ppermute | solution.py:389
  69.8 1.9 %collective-permute-start.4 = (f32[328,128]{1,0:T(8,128)S(1)}, f32[328,128]{1,0:T(8,128)S(1)}, u32[]{:S(2)}, u32[]{:S(2)}) collective-permute-start(f32[328,128]{1,0:T(8,128)S(1)} %get-tuple-element.34.refs_0_), channel_id=1, source_target_pairs={{0,1},{1,2},{2,3},{3,4},{4,5},{5,6},{6,7},{7,8},{8,9},{9,10},{10,1... | collective-permute-start | bytes 503816 | tf_op jit(solution)/shard_map/ppermute | solution.py:388
  71.7 0.9 collective-permute-done.5.refs_2_
  72.7 3.8 %collective-permute-done.4.refs_1_ = f32[328,128]{1,0:T(8,128)S(1)} collective-permute-done((f32[328,128]{1,0:T(8,128)S(1)}, f32[328,128]{1,0:T(8,128)S(1)}, u32[]{:S(2)}, u32[]{:S(2)}) %collective-permute-start.4) | collective-permute-done | bytes 167968 | tf_op jit(solution)/shard_map/ppermute | solution.py:388
  76.5 0.7 shard_map.79
  77.2 1.9 %collective-permute-start.7 = (f32[328,128]{1,0:T(8,128)S(1)}, f32[328,128]{1,0:T(8,128)S(1)}, u32[]{:S(2)}, u32[]{:S(2)}) collective-permute-start(f32[328,128]{1,0:T(8,128)S(1)} %get-tuple-element.36.refs_0_), channel_id=1, source_target_pairs={{1,0},{2,1},{3,2},{4,3},{5,4},{6,5},{7,6},{8,7},{9,8},{10,9},{11,1... | collective-permute-start | bytes 503816 | tf_op jit(solution)/shard_map/ppermute | solution.py:389
  79.1 2.4 %collective-permute-start.6 = (f32[328,128]{1,0:T(8,128)S(1)}, f32[328,128]{1,0:T(8,128)S(1)}, u32[]{:S(2)}, u32[]{:S(2)}) collective-permute-start(f32[328,128]{1,0:T(8,128)S(1)} %get-tuple-element.36.refs_0_), channel_id=1, source_target_pairs={{0,1},{1,2},{2,3},{3,4},{4,5},{5,6},{6,7},{7,8},{8,9},{9,10},{10,1... | collective-permute-start | bytes 503816 | tf_op jit(solution)/shard_map/ppermute | solution.py:388
  81.6 0.4 collective-permute-done.7.refs_2_
  82.0 3.8 %collective-permute-done.6.refs_1_ = f32[328,128]{1,0:T(8,128)S(1)} collective-permute-done((f32[328,128]{1,0:T(8,128)S(1)}, f32[328,128]{1,0:T(8,128)S(1)}, u32[]{:S(2)}, u32[]{:S(2)}) %collective-permute-start.6) | collective-permute-done | bytes 167968 | tf_op jit(solution)/shard_map/ppermute | solution.py:388
  85.8 1.0 shard_map.80
  86.8 27.2 %all_to_all.16.arrived_ref = f32[32,4,512]{2,1,0:T(4,128)S(1)} all-to-all(f32[32,4,512]{2,1,0:T(4,128)S(1)} %shard_map.80), channel_id=1, replica_groups=mesh['harm'=32,'slab'=16] {'harm'}, dimensions={0} | all-to-all | bytes 524288 | tf_op jit(solution)/shard_map/all_to_all | solution.py:415
  114.0 0.9 restore.1
  (1 shorter events, 0.0 us)
Async XLA Ops:
  3.1 37.0 %all-to-all-start = ((f32[32,4,384]{2,1,0:T(4,128)}), f32[32,4,384]{2,1,0:T(4,128)S(1)}, u32[]{:S(2)}, u32[]{:S(2)}) async-start(f32[32,4,384]{2,1,0:T(4,128)} %get-tuple-element.20), calls=%async_computation | async-start | bytes 393216 | tf_op jit(solution)/shard_map/all_to_all | solution.py:352
  40.2 4.5 %copy-start = (f32[5,5]{1,0:T(8,128)S(1)}, f32[5,5]{1,0:T(8,128)}, u32[]{:S(2)}) copy-start(f32[5,5]{1,0:T(8,128)} %param.10) | copy-start | bytes 304
  40.2 4.6 %copy-start.1 = (f32[5,5]{1,0:T(8,128)S(1)}, f32[5,5]{1,0:T(8,128)}, u32[]{:S(2)}) copy-start(f32[5,5]{1,0:T(8,128)} %param.11) | copy-start | bytes 304
  40.2 4.9 %collective-permute-start.1 = (f32[328,128]{1,0:T(8,128)S(1)}, f32[328,128]{1,0:T(8,128)S(1)}, u32[]{:S(2)}, u32[]{:S(2)}) collective-permute-start(f32[328,128]{1,0:T(8,128)S(1)} %get-tuple-element.24.refs_0_.refs_9_), channel_id=1, source_target_pairs={{1,0},{2,1},{3,2},{4,3},{5,4},{6,5},{7,6},{8,7},{9,8},{10,9},{11,1... | collective-permute-start | bytes 503816 | tf_op jit(solution)/shard_map/ppermute | solution.py:389
  42.3 6.7 %collective-permute-start = (f32[328,128]{1,0:T(8,128)S(1)}, f32[328,128]{1,0:T(8,128)S(1)}, u32[]{:S(2)}, u32[]{:S(2)}) collective-permute-start(f32[328,128]{1,0:T(8,128)S(1)} %get-tuple-element.24.refs_0_.refs_9_), channel_id=1, source_target_pairs={{0,1},{1,2},{2,3},{3,4},{4,5},{5,6},{6,7},{7,8},{8,9},{9,10},{10,1... | collective-permute-start | bytes 503816 | tf_op jit(solution)/shard_map/ppermute | solution.py:388
  49.8 16.5 %collective-permute-start.3 = (f32[328,128]{1,0:T(8,128)S(1)}, f32[328,128]{1,0:T(8,128)S(1)}, u32[]{:S(2)}, u32[]{:S(2)}) collective-permute-start(f32[328,128]{1,0:T(8,128)S(1)} %get-tuple-element.32.refs_9_), channel_id=1, source_target_pairs={{1,0},{2,1},{3,2},{4,3},{5,4},{6,5},{7,6},{8,7},{9,8},{10,9},{11,1... | collective-permute-start | bytes 503816 | tf_op jit(solution)/shard_map/ppermute | solution.py:389
  51.7 14.6 %collective-permute-start.2 = (f32[328,128]{1,0:T(8,128)S(1)}, f32[328,128]{1,0:T(8,128)S(1)}, u32[]{:S(2)}, u32[]{:S(2)}) collective-permute-start(f32[328,128]{1,0:T(8,128)S(1)} %get-tuple-element.32.refs_9_), channel_id=1, source_target_pairs={{0,1},{1,2},{2,3},{3,4},{4,5},{5,6},{6,7},{7,8},{8,9},{9,10},{10,1... | collective-permute-start | bytes 503816 | tf_op jit(solution)/shard_map/ppermute | solution.py:388
  67.0 5.7 %collective-permute-start.5 = (f32[328,128]{1,0:T(8,128)S(1)}, f32[328,128]{1,0:T(8,128)S(1)}, u32[]{:S(2)}, u32[]{:S(2)}) collective-permute-start(f32[328,128]{1,0:T(8,128)S(1)} %get-tuple-element.34.refs_0_), channel_id=1, source_target_pairs={{1,0},{2,1},{3,2},{4,3},{5,4},{6,5},{7,6},{8,7},{9,8},{10,9},{11,1... | collective-permute-start | bytes 503816 | tf_op jit(solution)/shard_map/ppermute | solution.py:389
  69.8 6.7 %collective-permute-start.4 = (f32[328,128]{1,0:T(8,128)S(1)}, f32[328,128]{1,0:T(8,128)S(1)}, u32[]{:S(2)}, u32[]{:S(2)}) collective-permute-start(f32[328,128]{1,0:T(8,128)S(1)} %get-tuple-element.34.refs_0_), channel_id=1, source_target_pairs={{0,1},{1,2},{2,3},{3,4},{4,5},{5,6},{6,7},{7,8},{8,9},{9,10},{10,1... | collective-permute-start | bytes 503816 | tf_op jit(solution)/shard_map/ppermute | solution.py:388
  77.2 4.8 %collective-permute-start.7 = (f32[328,128]{1,0:T(8,128)S(1)}, f32[328,128]{1,0:T(8,128)S(1)}, u32[]{:S(2)}, u32[]{:S(2)}) collective-permute-start(f32[328,128]{1,0:T(8,128)S(1)} %get-tuple-element.36.refs_0_), channel_id=1, source_target_pairs={{1,0},{2,1},{3,2},{4,3},{5,4},{6,5},{7,6},{8,7},{9,8},{10,9},{11,1... | collective-permute-start | bytes 503816 | tf_op jit(solution)/shard_map/ppermute | solution.py:389
  79.1 6.7 %collective-permute-start.6 = (f32[328,128]{1,0:T(8,128)S(1)}, f32[328,128]{1,0:T(8,128)S(1)}, u32[]{:S(2)}, u32[]{:S(2)}) collective-permute-start(f32[328,128]{1,0:T(8,128)S(1)} %get-tuple-element.36.refs_0_), channel_id=1, source_target_pairs={{0,1},{1,2},{2,3},{3,4},{4,5},{5,6},{6,7},{7,8},{8,9},{9,10},{10,1... | collective-permute-start | bytes 503816 | tf_op jit(solution)/shard_map/ppermute | solution.py:388

commit v4 on v3

--- a/solution.py
+++ b/solution.py
@@ -111,12 +111,12 @@
 
 def section_kernel(*refs, stage, cell_count):
     last = stage == len(SECTION_RATES) - 1
-    own_ref, left_ref, right_ref, mean_ref, omega_ref, wall_ref, jac_ref, radius_ref = refs[:8]
-    refs = refs[8:]
+    parity_ref, own_ref, core_ref, chip_ref, *refs = refs
+    mean_ref, omega_ref, wall_ref, jac_ref, radius_ref, *refs = refs
     if stage == 0:
         outs = refs
     elif stage == 1:
-        speed_ref, own_res, left_res, right_res, mean_res, *outs = refs
+        speed_ref, own_res, core_res, chip_res, mean_res, *outs = refs
         h0_ref, m0_ref = own_ref, mean_ref
     else:
         speed_ref, h0_ref, m0_ref, *outs = refs
@@ -151,11 +151,11 @@
         time_step = COURANT / (1.0 + jnp.sqrt(speed_total / cell_count))
         time_step = jnp.broadcast_to(time_step, (C1, LANES))
         step = SECTION_RATES[stage] * time_step
-    blocks = [(left_ref, None), (own_ref, None), (right_ref, None)]
+    own, core, chip = (own_ref, None), (core_ref, None), (chip_ref, None)
     mean_block = (mean_ref, None)
     if stage == 1:
         first = SECTION_RATES[0] * time_step
-        blocks = [(left_ref, left_res), (own_ref, own_res), (right_ref, right_res)]
+        own, core, chip = (own_ref, own_res), (core_ref, core_res), (chip_ref, chip_res)
         mean_block = (mean_ref, mean_res)
 
     def load(block, row, count=C1):
@@ -165,15 +165,21 @@
             value = value + first[:count] * residual[row : row + count, :]
         return value
 
+    on_first = parity_ref[0] == 0
+
+    def sides(row, count=C1):
+        paired, other = load(core, row, count), load(chip, row, count)
+        return jnp.where(on_first, other, paired), jnp.where(on_first, paired, other)
+
     def column(part, var):
-        row = h_row(part, var, 0)
-        return [load(block, row + C1 * cell) for block in blocks for cell in range(CELLS)]
+        rows = [h_row(part, var, cell) for cell in range(CELLS)]
+        left, right = zip(*[sides(row) for row in rows])
+        return [*left, *[load(own, row) for row in rows], *right]
 
     inv_radius = 1.0 / splat(radius_ref, 0)
 
     harm = [[column(part, var) for var in range(VARS)] for part in range(2)]
-    left_mean = unpack_mean(load(blocks[0], H_ROWS, 8))
-    right_mean = unpack_mean(load(blocks[2], H_ROWS, 8))
+    left_mean, right_mean = [unpack_mean(packed) for packed in sides(H_ROWS, 8)]
     mean = []
     for var in range(VARS):
         own_mean = [load(mean_block, m_row(var, cell)) for cell in range(CELLS)]
@@ -384,10 +390,15 @@
     speeds = lax.all_to_all(speed, "slab", 0, 0, tiled=True)
     cell_count = CELLS * slab_count * plane_count
 
+    core_pairs = [(i, i ^ 1) for i in range(slab_count)]
+    chip_pairs = [
+        pair for i in range(1, slab_count - 1, 2) for pair in ((i, i + 1), (i + 1, i))
+    ]
+
     def beside(state):
-        left = lax.ppermute(state, "slab", [(i, i + 1) for i in range(slab_count - 1)])
-        right = lax.ppermute(state, "slab", [(i + 1, i) for i in range(slab_count - 1)])
-        return state, left, right
+        core = lax.ppermute(state, "slab", core_pairs)
+        chip = lax.ppermute(state, "slab", chip_pairs)
+        return state, core, chip
 
     def section(stage, *operands):
         if stage == len(SECTION_RATES) - 1:
@@ -399,11 +410,12 @@
         return pl.pallas_call(
             functools.partial(section_kernel, stage=stage, cell_count=cell_count),
             out_shape=shapes,
-            in_specs=[VMEM] * len(operands),
+            in_specs=[SMEM] + [VMEM] * len(operands),
             out_specs=specs,
             scratch_shapes=scratch,
-        )(*held(*operands))
-
+        )(parity, *held(*operands))
+
+    parity = (lax.axis_index("slab") % 2).astype(jnp.int32).reshape(1)
     fixed = (omega, wall, jac, radius)
     start_blocks = beside(start)
     residual, mean_residual = section(0, *start_blocks, mean_start, *fixed)

time: 115 us -> 112 us (0.974)
  the two profiles are of different devices: /device:TPU:6 before, /device:TPU:7 now
where the time goes in v4:
time: 112 us; the launch traced here: 111 us
  starting transfers between devices  43.7 us (39%)
  blocking collectives  35.6 us (32%)
  waiting for transfers between devices  21.7 us (19%)
  Pallas kernels  7.09 us (6%)
  between operations  1.43 us (1%)
    all_to_all x1, blocking collectives, shards(): back = lax.all_to_all(result, 'harm', 0, 0, tiled=True)  25.3 us
    ppermute x4, starting transfers between devices, beside(): chip = lax.ppermute(state, 'slab', chip_pairs)  18.4 us
    all_to_all x1, starting transfers between devices, shards(): arrived = lax.all_to_all(sends, 'harm', 0, 0, tiled=True)  17.7 us
    all_to_all x1, waiting for transfers between devices, shards(): arrived = lax.all_to_all(sends, 'harm', 0, 0, tiled=True)  16 us
    all_to_all x1, blocking collectives, shards(): speeds = lax.all_to_all(speed, 'slab', 0, 0, tiled=True)  10.3 us
    ppermute x4, starting transfers between devices, beside(): core = lax.ppermute(state, 'slab', core_pairs)  7.68 us
    ppermute x4, waiting for transfers between devices, beside(): chip = lax.ppermute(state, 'slab', chip_pairs)  5.68 us
    pallas_call x4, Pallas kernels, section(): pl.pallas_call(functools.partial(section_kernel, stage=stage, cell_count=...  3.21 us
  transfers between devices with their start and end apart: 9, of which 4 were waited for; matrix products, arithmetic and copies ran while one was open for 0% of the time, Pallas kernels for 1%

profile of v4, /device:TPU:7, one launch (start us, length us, event | category | flops | bytes accessed | tf_op | source)
XLA Modules:
  0.0 110.5 jit_solution(3932197363259498824)
XLA Ops:
  1.3 1.8 %pack.1 = (f32[32,4,384]{2,1,0:T(4,128)}, f32[8,128]{1,0:T(8,128)S(1)}) custom-call(f32[1,2,5,2,2048]{4,3,2,1,0:T(2,128)} %harm_ref.1, s32[1]{0:T(128)S(6)} %copy.8.freq_ref), custom_call_target="tpu_custom_call" | custom-call | tf_op jit(solution)/shard_map/pack/pallas_call | solution.py:350
  3.1 17.7 %all-to-all-start = ((f32[32,4,384]{2,1,0:T(4,128)}), f32[32,4,384]{2,1,0:T(4,128)S(1)}, u32[]{:S(2)}, u32[]{:S(2)}) async-start(f32[32,4,384]{2,1,0:T(4,128)} %get-tuple-element.20), calls=%async_computation | async-start | bytes 393216 | tf_op jit(solution)/shard_map/all_to_all | solution.py:358
  20.8 1.0 prepare.1
  21.8 16.0 %all-to-all-done.arrived_ref = f32[32,4,384]{2,1,0:T(4,128)S(1)} async-done(((f32[32,4,384]{2,1,0:T(4,128)}), f32[32,4,384]{2,1,0:T(4,128)S(1)}, u32[]{:S(2)}, u32[]{:S(2)}) %all-to-all-start) | async-done | bytes 196640 | tf_op jit(solution)/shard_map/all_to_all | solution.py:358
  37.8 0.1 unpack.1
  37.9 6.3 %collective-permute-start.1 = (f32[328,128]{1,0:T(8,128)S(1)}, f32[328,128]{1,0:T(8,128)S(1)}, u32[]{:S(2)}, u32[]{:S(2)}) collective-permute-start(f32[328,128]{1,0:T(8,128)S(1)} %get-tuple-element.24.refs_1_.refs_10_), channel_id=1, source_target_pairs={{1,2},{2,1},{3,4},{4,3},{5,6},{6,5},{7,8},{8,7},{9,10},{10,9},{11,... | collective-permute-start | bytes 503816 | tf_op jit(solution)/shard_map/ppermute | solution.py:400
  44.2 1.9 %collective-permute-start = (f32[328,128]{1,0:T(8,128)S(1)}, f32[328,128]{1,0:T(8,128)S(1)}, u32[]{:S(2)}, u32[]{:S(2)}) collective-permute-start(f32[328,128]{1,0:T(8,128)S(1)} %get-tuple-element.24.refs_1_.refs_10_), channel_id=1, source_target_pairs={{0,1},{1,0},{2,3},{3,2},{4,5},{5,4},{6,7},{7,6},{8,9},{9,8},{10,11... | collective-permute-start | bytes 503816 | tf_op jit(solution)/shard_map/ppermute | solution.py:399
  46.2 0.0 copy-start
  46.2 0.0 copy-start.1
  46.2 0.7 copy-done
  46.9 0.1 reshape.56
  47.0 0.0 copy-done.1
  47.0 0.1 reshape.57
  47.0 0.1 maximum_bitcast_fusion
  47.1 1.3 %collective-permute-done.1.refs_3_ = f32[328,128]{1,0:T(8,128)S(1)} collective-permute-done((f32[328,128]{1,0:T(8,128)S(1)}, f32[328,128]{1,0:T(8,128)S(1)}, u32[]{:S(2)}, u32[]{:S(2)}) %collective-permute-start.1) | collective-permute-done | bytes 167968 | tf_op jit(solution)/shard_map/ppermute | solution.py:400
  48.5 0.0 collective-permute-done.refs_2_
  48.5 0.1 broadcast_in_dim.8.refs_7_
  48.5 0.7 shard_map.77
  49.3 3.9 %collective-permute-start.3 = (f32[328,128]{1,0:T(8,128)S(1)}, f32[328,128]{1,0:T(8,128)S(1)}, u32[]{:S(2)}, u32[]{:S(2)}) collective-permute-start(f32[328,128]{1,0:T(8,128)S(1)} %get-tuple-element.32.refs_10_), channel_id=1, source_target_pairs={{1,2},{2,1},{3,4},{4,3},{5,6},{6,5},{7,8},{8,7},{9,10},{10,9},{11,... | collective-permute-start | bytes 503816 | tf_op jit(solution)/shard_map/ppermute | solution.py:400
  53.2 1.9 %collective-permute-start.2 = (f32[328,128]{1,0:T(8,128)S(1)}, f32[328,128]{1,0:T(8,128)S(1)}, u32[]{:S(2)}, u32[]{:S(2)}) collective-permute-start(f32[328,128]{1,0:T(8,128)S(1)} %get-tuple-element.32.refs_10_), channel_id=1, source_target_pairs={{0,1},{1,0},{2,3},{3,2},{4,5},{5,4},{6,7},{7,6},{8,9},{9,8},{10,11... | collective-permute-start | bytes 503816 | tf_op jit(solution)/shard_map/ppermute | solution.py:399
  55.1 10.3 %all_to_all.15.refs_9_ = f32[16,1,128]{2,1,0:T(1,128)S(1)} all-to-all(f32[16,1,128]{2,1,0:T(1,128)S(1)} %get-tuple-element.31), channel_id=1, replica_groups=mesh['harm'=32,'slab'=16] {'slab'}, dimensions={0} | all-to-all | bytes 16384 | tf_op jit(solution)/shard_map/all_to_all | solution.py:390
  65.4 0.0 collective-permute-done.3.refs_12_
  65.4 0.0 collective-permute-done.2.refs_11_
  65.4 0.8 shard_map.78
  66.2 3.6 %collective-permute-start.5 = (f32[328,128]{1,0:T(8,128)S(1)}, f32[328,128]{1,0:T(8,128)S(1)}, u32[]{:S(2)}, u32[]{:S(2)}) collective-permute-start(f32[328,128]{1,0:T(8,128)S(1)} %get-tuple-element.34.refs_1_), channel_id=1, source_target_pairs={{1,2},{2,1},{3,4},{4,3},{5,6},{6,5},{7,8},{8,7},{9,10},{10,9},{11,... | collective-permute-start | bytes 503816 | tf_op jit(solution)/shard_map/ppermute | solution.py:400
  69.8 1.9 %collective-permute-start.4 = (f32[328,128]{1,0:T(8,128)S(1)}, f32[328,128]{1,0:T(8,128)S(1)}, u32[]{:S(2)}, u32[]{:S(2)}) collective-permute-start(f32[328,128]{1,0:T(8,128)S(1)} %get-tuple-element.34.refs_1_), channel_id=1, source_target_pairs={{0,1},{1,0},{2,3},{3,2},{4,5},{5,4},{6,7},{7,6},{8,9},{9,8},{10,11... | collective-permute-start | bytes 503816 | tf_op jit(solution)/shard_map/ppermute | solution.py:399
  71.7 2.9 %collective-permute-done.5.refs_3_ = f32[328,128]{1,0:T(8,128)S(1)} collective-permute-done((f32[328,128]{1,0:T(8,128)S(1)}, f32[328,128]{1,0:T(8,128)S(1)}, u32[]{:S(2)}, u32[]{:S(2)}) %collective-permute-start.5) | collective-permute-done | bytes 167968 | tf_op jit(solution)/shard_map/ppermute | solution.py:400
  74.6 0.0 collective-permute-done.4.refs_2_
  74.6 0.7 shard_map.79
  75.4 4.5 %collective-permute-start.7 = (f32[328,128]{1,0:T(8,128)S(1)}, f32[328,128]{1,0:T(8,128)S(1)}, u32[]{:S(2)}, u32[]{:S(2)}) collective-permute-start(f32[328,128]{1,0:T(8,128)S(1)} %get-tuple-element.36.refs_1_), channel_id=1, source_target_pairs={{1,2},{2,1},{3,4},{4,3},{5,6},{6,5},{7,8},{8,7},{9,10},{10,9},{11,... | collective-permute-start | bytes 503816 | tf_op jit(solution)/shard_map/ppermute | solution.py:400
  79.9 1.9 %collective-permute-start.6 = (f32[328,128]{1,0:T(8,128)S(1)}, f32[328,128]{1,0:T(8,128)S(1)}, u32[]{:S(2)}, u32[]{:S(2)}) collective-permute-start(f32[328,128]{1,0:T(8,128)S(1)} %get-tuple-element.36.refs_1_), channel_id=1, source_target_pairs={{0,1},{1,0},{2,3},{3,2},{4,5},{5,4},{6,7},{7,6},{8,9},{9,8},{10,11... | collective-permute-start | bytes 503816 | tf_op jit(solution)/shard_map/ppermute | solution.py:399
  81.8 1.5 %collective-permute-done.7.refs_3_ = f32[328,128]{1,0:T(8,128)S(1)} collective-permute-done((f32[328,128]{1,0:T(8,128)S(1)}, f32[328,128]{1,0:T(8,128)S(1)}, u32[]{:S(2)}, u32[]{:S(2)}) %collective-permute-start.7) | collective-permute-done | bytes 167968 | tf_op jit(solution)/shard_map/ppermute | solution.py:400
  83.3 0.0 collective-permute-done.6.refs_2_
  83.3 1.0 shard_map.80
  84.3 25.3 %all_to_all.16.arrived_ref = f32[32,4,512]{2,1,0:T(4,128)S(1)} all-to-all(f32[32,4,512]{2,1,0:T(4,128)S(1)} %shard_map.80), channel_id=1, replica_groups=mesh['harm'=32,'slab'=16] {'harm'}, dimensions={0} | all-to-all | bytes 524288 | tf_op jit(solution)/shard_map/all_to_all | solution.py:427
  109.6 0.9 restore.1
  (1 shorter events, 0.0 us)
Async XLA Ops:
  3.1 34.7 %all-to-all-start = ((f32[32,4,384]{2,1,0:T(4,128)}), f32[32,4,384]{2,1,0:T(4,128)S(1)}, u32[]{:S(2)}, u32[]{:S(2)}) async-start(f32[32,4,384]{2,1,0:T(4,128)} %get-tuple-element.20), calls=%async_computation | async-start | bytes 393216 | tf_op jit(solution)/shard_map/all_to_all | solution.py:358
  37.9 10.5 %collective-permute-start.1 = (f32[328,128]{1,0:T(8,128)S(1)}, f32[328,128]{1,0:T(8,128)S(1)}, u32[]{:S(2)}, u32[]{:S(2)}) collective-permute-start(f32[328,128]{1,0:T(8,128)S(1)} %get-tuple-element.24.refs_1_.refs_10_), channel_id=1, source_target_pairs={{1,2},{2,1},{3,4},{4,3},{5,6},{6,5},{7,8},{8,7},{9,10},{10,9},{11,... | collective-permute-start | bytes 503816 | tf_op jit(solution)/shard_map/ppermute | solution.py:400
  44.2 4.2 %collective-permute-start = (f32[328,128]{1,0:T(8,128)S(1)}, f32[328,128]{1,0:T(8,128)S(1)}, u32[]{:S(2)}, u32[]{:S(2)}) collective-permute-start(f32[328,128]{1,0:T(8,128)S(1)} %get-tuple-element.24.refs_1_.refs_10_), channel_id=1, source_target_pairs={{0,1},{1,0},{2,3},{3,2},{4,5},{5,4},{6,7},{7,6},{8,9},{9,8},{10,11... | collective-permute-start | bytes 503816 | tf_op jit(solution)/shard_map/ppermute | solution.py:399
  46.2 0.7 copy-start
  46.2 0.8 copy-start.1
  49.3 16.1 %collective-permute-start.3 = (f32[328,128]{1,0:T(8,128)S(1)}, f32[328,128]{1,0:T(8,128)S(1)}, u32[]{:S(2)}, u32[]{:S(2)}) collective-permute-start(f32[328,128]{1,0:T(8,128)S(1)} %get-tuple-element.32.refs_10_), channel_id=1, source_target_pairs={{1,2},{2,1},{3,4},{4,3},{5,6},{6,5},{7,8},{8,7},{9,10},{10,9},{11,... | collective-permute-start | bytes 503816 | tf_op jit(solution)/shard_map/ppermute | solution.py:400
  53.2 12.2 %collective-permute-start.2 = (f32[328,128]{1,0:T(8,128)S(1)}, f32[328,128]{1,0:T(8,128)S(1)}, u32[]{:S(2)}, u32[]{:S(2)}) collective-permute-start(f32[328,128]{1,0:T(8,128)S(1)} %get-tuple-element.32.refs_10_), channel_id=1, source_target_pairs={{0,1},{1,0},{2,3},{3,2},{4,5},{5,4},{6,7},{7,6},{8,9},{9,8},{10,11... | collective-permute-start | bytes 503816 | tf_op jit(solution)/shard_map/ppermute | solution.py:399
  66.2 8.5 %collective-permute-start.5 = (f32[328,128]{1,0:T(8,128)S(1)}, f32[328,128]{1,0:T(8,128)S(1)}, u32[]{:S(2)}, u32[]{:S(2)}) collective-permute-start(f32[328,128]{1,0:T(8,128)S(1)} %get-tuple-element.34.refs_1_), channel_id=1, source_target_pairs={{1,2},{2,1},{3,4},{4,3},{5,6},{6,5},{7,8},{8,7},{9,10},{10,9},{11,... | collective-permute-start | bytes 503816 | tf_op jit(solution)/shard_map/ppermute | solution.py:400
  69.8 4.8 %collective-permute-start.4 = (f32[328,128]{1,0:T(8,128)S(1)}, f32[328,128]{1,0:T(8,128)S(1)}, u32[]{:S(2)}, u32[]{:S(2)}) collective-permute-start(f32[328,128]{1,0:T(8,128)S(1)} %get-tuple-element.34.refs_1_), channel_id=1, source_target_pairs={{0,1},{1,0},{2,3},{3,2},{4,5},{5,4},{6,7},{7,6},{8,9},{9,8},{10,11... | collective-permute-start | bytes 503816 | tf_op jit(solution)/shard_map/ppermute | solution.py:399
  75.4 7.9 %collective-permute-start.7 = (f32[328,128]{1,0:T(8,128)S(1)}, f32[328,128]{1,0:T(8,128)S(1)}, u32[]{:S(2)}, u32[]{:S(2)}) collective-permute-start(f32[328,128]{1,0:T(8,128)S(1)} %get-tuple-element.36.refs_1_), channel_id=1, source_target_pairs={{1,2},{2,1},{3,4},{4,3},{5,6},{6,5},{7,8},{8,7},{9,10},{10,9},{11,... | collective-permute-start | bytes 503816 | tf_op jit(solution)/shard_map/ppermute | solution.py:400
  79.9 3.4 %collective-permute-start.6 = (f32[328,128]{1,0:T(8,128)S(1)}, f32[328,128]{1,0:T(8,128)S(1)}, u32[]{:S(2)}, u32[]{:S(2)}) collective-permute-start(f32[328,128]{1,0:T(8,128)S(1)} %get-tuple-element.36.refs_1_), channel_id=1, source_target_pairs={{0,1},{1,0},{2,3},{3,2},{4,5},{5,4},{6,7},{7,6},{8,9},{9,8},{10,11... | collective-permute-start | bytes 503816 | tf_op jit(solution)/shard_map/ppermute | solution.py:399

commit v5 on v4

--- a/solution.py
+++ b/solution.py
@@ -73,9 +73,17 @@
 
 
 def prepare_kernel(
-    mean_ref, wall_ref, position_ref, token_ref, mean_out, wall_out, packed_out, speed_out, rows_ref
+    mean_ref, wall_ref, jac_x_ref, jac_y_ref, position_ref, token_ref,
+    mean_out, wall_out, packed_out, speed_out, jac_out, rows_ref
 ):
     del token_ref
+    for base, matrix_ref in ((0, jac_x_ref), (VARS * VARS, jac_y_ref)):
+        for a in range(VARS):
+            for b in range(VARS):
+                row = base + VARS * a + b
+                jac_out[row : row + 1, :] = jnp.broadcast_to(
+                    matrix_ref[a : a + 1, b : b + 1], (1, LANES)
+                )
     for cell in range(CELLS):
         for c1 in range(C1):
             cols = slice(c1 * LANES, (c1 + 1) * LANES)
@@ -99,8 +107,8 @@
     )
 
 
-def unpack_kernel(arrived_ref, packed_ref, speed_ref, state_out, omega_out, speed_out, rows_ref):
-    speed_out[...] = speed_ref[...]
+def unpack_kernel(arrived_ref, packed_ref, speed_ref, state_out, omega_out, rows_ref):
+    del speed_ref
     for k in range(32):
         rows_ref[4 * k : 4 * k + 4, :] = arrived_ref[k]
     turned = rows_ref[...].T
@@ -113,13 +121,23 @@
     last = stage == len(SECTION_RATES) - 1
     parity_ref, own_ref, core_ref, chip_ref, *refs = refs
     mean_ref, omega_ref, wall_ref, jac_ref, radius_ref, *refs = refs
+    if stage < 2:
+        speed_ref, beside_ref, *refs = refs
+        speed = speed_ref[...] + beside_ref[...]
     if stage == 0:
-        outs = refs
+        *outs, speed_out = refs
+        speed_out[...] = speed
     elif stage == 1:
-        speed_ref, own_res, core_res, chip_res, mean_res, *outs = refs
+        own_res, core_res, chip_res, mean_res, *outs, step_out = refs
         h0_ref, m0_ref = own_ref, mean_ref
+        time_step = COURANT / (1.0 + jnp.sqrt(speed / cell_count))
+        step_out[...] = time_step
     else:
-        speed_ref, h0_ref, m0_ref, *outs = refs
+        step_ref, h0_ref, m0_ref, *outs = refs
+        time_step = step_ref[...]
+    if stage:
+        time_step = jnp.concatenate([time_step, time_step], axis=0)
+
     lane = lax.broadcasted_iota(jnp.int32, (C1, LANES), 1)
     even = (lane // 2) % 2 == 0
 
@@ -147,9 +165,6 @@
 
     omega = splat(omega_ref, 0)
     if stage:
-        speed_total = jnp.sum(speed_ref[...], axis=0)
-        time_step = COURANT / (1.0 + jnp.sqrt(speed_total / cell_count))
-        time_step = jnp.broadcast_to(time_step, (C1, LANES))
         step = SECTION_RATES[stage] * time_step
     own, core, chip = (own_ref, None), (core_ref, None), (chip_ref, None)
     mean_block = (mean_ref, None)
@@ -357,38 +372,41 @@
     )(harmonics, freq_index)
     arrived = lax.all_to_all(sends, "harm", 0, 0, tiled=True)
 
-    mean_start, wall, packed, speed = pl.pallas_call(
+    mean_start, wall, packed, speed, jac = pl.pallas_call(
         prepare_kernel,
         out_shape=(
             kept(M_ROWS, LANES),
             kept(W_ROWS, LANES),
             kept(8, LANES),
-            kept(slab_count, 1, LANES),
+            kept(8, LANES),
+            kept(2 * VARS * VARS, LANES),
         ),
-        in_specs=[VMEM, VMEM, SMEM, VMEM],
-        out_specs=(VMEM,) * 4,
+        in_specs=[VMEM] * 4 + [SMEM, VMEM],
+        out_specs=(VMEM,) * 5,
         scratch_shapes=rows_scratch(M_ROWS + W_ROWS, LANES),
         name="prepare",
-    )(mean_flow, wall_mask, position.astype(jnp.int32).reshape(1), *held(token))
-    mean_start, jacobian_x, jacobian_y = lax.optimization_barrier(
-        (mean_start, jacobian_x, jacobian_y)
+    )(
+        mean_flow, wall_mask, jacobian_x, jacobian_y, position.astype(jnp.int32).reshape(1),
+        *held(token)
     )
+
+    def crossed(value, reach):
+        return lax.ppermute(value, "slab", [(i, i ^ reach) for i in range(slab_count)])
+
+    cell_count = CELLS * slab_count * plane_count
+    for reach in (1, 2):
+        speed = speed + crossed(speed, reach)
     radial = 2 * position + jnp.arange(LANES) % 2
     radius = (HUB_RADIUS + (radial.astype(jnp.float32) + 0.5) / NZ).reshape(1, LANES)
-    jac = jnp.concatenate([jacobian_x.reshape(-1, 1), jacobian_y.reshape(-1, 1)])
-    jac = jnp.broadcast_to(jac, (2 * VARS * VARS, LANES))
-
-    start, omega, speed = pl.pallas_call(
+
+    start, omega = pl.pallas_call(
         unpack_kernel,
-        out_shape=(kept(H_ROWS + 8, LANES), kept(8, LANES), kept(slab_count, 1, LANES)),
+        out_shape=(kept(H_ROWS + 8, LANES), kept(8, LANES)),
         in_specs=[VMEM] * 3,
-        out_specs=(VMEM,) * 3,
+        out_specs=(VMEM,) * 2,
         scratch_shapes=rows_scratch(LANES, 384),
         name="unpack",
     )(*held(arrived, packed, speed))
-
-    speeds = lax.all_to_all(speed, "slab", 0, 0, tiled=True)
-    cell_count = CELLS * slab_count * plane_count
 
     core_pairs = [(i, i ^ 1) for i in range(slab_count)]
     chip_pairs = [
@@ -401,29 +419,32 @@
         return state, core, chip
 
     def section(stage, *operands):
+        shapes = [kept(H_ROWS + 8, LANES), kept(M_ROWS, LANES), kept(8, LANES)]
+        scratch = []
         if stage == len(SECTION_RATES) - 1:
-            shapes, scratch = kept(32, 4, 512), rows_scratch(512, LANES)
-            specs = VMEM
-        else:
-            shapes, scratch = (kept(H_ROWS + 8, LANES), kept(M_ROWS, LANES)), []
-            specs = (VMEM, VMEM)
+            shapes, scratch = [kept(32, 4, 512)], rows_scratch(512, LANES)
+        elif stage == len(SECTION_RATES) - 2:
+            del shapes[2]
         return pl.pallas_call(
             functools.partial(section_kernel, stage=stage, cell_count=cell_count),
             out_shape=shapes,
             in_specs=[SMEM] + [VMEM] * len(operands),
-            out_specs=specs,
+            out_specs=[VMEM] * len(shapes),
             scratch_shapes=scratch,
         )(parity, *held(*operands))
 
     parity = (lax.axis_index("slab") % 2).astype(jnp.int32).reshape(1)
     fixed = (omega, wall, jac, radius)
-    start_blocks = beside(start)
-    residual, mean_residual = section(0, *start_blocks, mean_start, *fixed)
-    state, mean_now = section(
-        1, *start_blocks, mean_start, *fixed, speeds, *beside(residual), mean_residual
+    blocks = beside(start)
+    speed_beside = crossed(speed, 4)
+    residual, mean_residual, speed = section(0, *blocks, mean_start, *fixed, speed, speed_beside)
+    residual_blocks = beside(residual)
+    speed_beside = crossed(speed, 8)
+    state, mean_now, step = section(
+        1, *blocks, mean_start, *fixed, speed, speed_beside, *residual_blocks, mean_residual
     )
-    state, mean_now = section(2, *beside(state), mean_now, *fixed, speeds, start, mean_start)
-    result = section(3, *beside(state), mean_now, *fixed, speeds, start, mean_start)
+    state, mean_now = section(2, *beside(state), mean_now, *fixed, step, start, mean_start)
+    (result,) = section(3, *beside(state), mean_now, *fixed, step, start, mean_start)
     back = lax.all_to_all(result, "harm", 0, 0, tiled=True)
     return pl.pallas_call(
         restore_kernel,

time: 112 us -> 113 us (level)
  starting transfers between devices: 43.7 us -> 58.2 us
  blocking collectives: 35.6 us -> 25.8 us
  waiting for transfers between devices: 21.7 us -> 18.3 us
    ppermute x0 -> x4, starting transfers between devices: none -> 13.3 us  [crossed(): lax.ppermute(value, 'slab', [(i, i ^ reach) for i in range(slab_count)])]
    all_to_all x1 -> x0, blocking collectives: 10.3 us -> none  [shards(): speeds = lax.all_to_all(speed, 'slab', 0, 0, tiled=True)]
    all_to_all x1, waiting for transfers between devices: 16 us -> 7.33 us  [shards(): arrived = lax.all_to_all(sends, 'harm', 0, 0, tiled=True)]
    ppermute x0 -> x4, waiting for transfers between devices: none -> 5.42 us  [crossed(): lax.ppermute(value, 'slab', [(i, i ^ reach) for i in range(slab_count)])]
    ppermute x4, starting transfers between devices: 18.4 us -> 19.6 us  [beside(): chip = lax.ppermute(state, 'slab', chip_pairs)]
  transfers between devices with their start and end apart: 9 -> 13, of which waited for: 4 -> 7; matrix products, arithmetic and copies ran while one was open for 0% -> 0% of each run, Pallas kernels for 1% -> 1%
where the time goes in v5:
time: 113 us; the launch traced here: 111 us
  starting transfers between devices  58.2 us (52%)
  blocking collectives  25.8 us (23%)
  waiting for transfers between devices  18.3 us (16%)
  Pallas kernels  7.14 us (6%)
  between operations  1.45 us (1%)
    all_to_all x1, blocking collectives, shards(): back = lax.all_to_all(result, 'harm', 0, 0, tiled=True)  25.8 us
    ppermute x4, starting transfers between devices, beside(): chip = lax.ppermute(state, 'slab', chip_pairs)  19.6 us
    all_to_all x1, starting transfers between devices, shards(): arrived = lax.all_to_all(sends, 'harm', 0, 0, tiled=True)  17.7 us
    ppermute x4, starting transfers between devices, crossed(): lax.ppermute(value, 'slab', [(i, i ^ reach) for i in range(slab_count)])  13.3 us
    ppermute x4, starting transfers between devices, beside(): core = lax.ppermute(state, 'slab', core_pairs)  7.68 us
    all_to_all x1, waiting for transfers between devices, shards(): arrived = lax.all_to_all(sends, 'harm', 0, 0, tiled=True)  7.33 us
    ppermute x4, waiting for transfers between devices, beside(): chip = lax.ppermute(state, 'slab', chip_pairs)  5.55 us
    ppermute x4, waiting for transfers between devices, crossed(): lax.ppermute(value, 'slab', [(i, i ^ reach) for i in range(slab_count)])  5.42 us
  transfers between devices with their start and end apart: 13, of which 7 were waited for; matrix products, arithmetic and copies ran while one was open for 0% of the time, Pallas kernels for 1%

profile of v5, /device:TPU:7, one launch (start us, length us, event | category | flops | bytes accessed | tf_op | source)
XLA Modules:
  0.0 111.0 jit_solution(4847558456516027355)
XLA Ops:
  1.3 1.8 %pack.1 = (f32[32,4,384]{2,1,0:T(4,128)}, f32[8,128]{1,0:T(8,128)S(1)}) custom-call(f32[1,2,5,2,2048]{4,3,2,1,0:T(2,128)} %harm_ref.1, s32[1]{0:T(128)S(6)} %copy.8.freq_ref), custom_call_target="tpu_custom_call" | custom-call | tf_op jit(solution)/shard_map/pack/pallas_call | solution.py:365
  3.1 17.7 %all-to-all-start = ((f32[32,4,384]{2,1,0:T(4,128)}), f32[32,4,384]{2,1,0:T(4,128)S(1)}, u32[]{:S(2)}, u32[]{:S(2)}) async-start(f32[32,4,384]{2,1,0:T(4,128)} %get-tuple-element.19), calls=%async_computation | async-start | bytes 393216 | tf_op jit(solution)/shard_map/all_to_all | solution.py:373
  20.8 1.1 %prepare.1 = (f32[160,128]{1,0:T(8,128)S(1)}, f32[32,128]{1,0:T(8,128)S(1)}, f32[8,128]{1,0:T(8,128)S(1)}, f32[8,128]{1,0:T(8,128)S(1)}, f32[50,128]{1,0:T(8,128)S(1)}) custom-call(f32[5,2,2048]{2,1,0:T(2,128)} %mean_ref.1, s32[2,2048]{1,0:T(2,128)} %wall_ref.1, f32[5,5]{1,0:T(8,128)} %jac_x_ref.1, f32[5,5]{1,0:T(8,128)} %jac_y_ref.1, ...), custom_call_target="tpu_custom_call" | custom-call | tf_op jit(solution)/shard_map/prepare/pallas_call | solution.py:375
  21.9 3.1 %collective-permute-start = (f32[8,128]{1,0:T(8,128)S(1)}, f32[8,128]{1,0:T(8,128)S(1)}, u32[]{:S(2)}, u32[]{:S(2)}) collective-permute-start(f32[8,128]{1,0:T(8,128)S(1)} %get-tuple-element.22), channel_id=1, source_target_pairs={{0,1},{1,0},{2,3},{3,2},{4,5},{5,4},{6,7},{7,6},{8,9},{9,8},{10,11... | collective-permute-start | bytes 12296 | tf_op jit(solution)/shard_map/ppermute | solution.py:394
  25.0 0.8 collective-permute-done
  25.8 2.4 %collective-permute-start.1 = (f32[8,128]{1,0:T(8,128)S(1)}, f32[8,128]{1,0:T(8,128)S(1)}, u32[]{:S(2)}, u32[]{:S(2)}) collective-permute-start(f32[8,128]{1,0:T(8,128)S(1)} %add.57), channel_id=1, source_target_pairs={{0,2},{1,3},{2,0},{3,1},{4,6},{5,7},{6,4},{7,5},{8,10},{9,11},{10,... | collective-permute-start | bytes 12296 | tf_op jit(solution)/shard_map/ppermute | solution.py:394
  28.3 2.2 %collective-permute-done.1 = f32[8,128]{1,0:T(8,128)S(1)} collective-permute-done((f32[8,128]{1,0:T(8,128)S(1)}, f32[8,128]{1,0:T(8,128)S(1)}, u32[]{:S(2)}, u32[]{:S(2)}) %collective-permute-start.1) | collective-permute-done | bytes 4128 | tf_op jit(solution)/shard_map/ppermute | solution.py:394
  30.5 7.3 %all-to-all-done.arrived_ref = f32[32,4,384]{2,1,0:T(4,128)S(1)} async-done(((f32[32,4,384]{2,1,0:T(4,128)}), f32[32,4,384]{2,1,0:T(4,128)S(1)}, u32[]{:S(2)}, u32[]{:S(2)}) %all-to-all-start) | async-done | bytes 196640 | tf_op jit(solution)/shard_map/all_to_all | solution.py:373
  37.8 0.1 unpack.1
  37.9 6.3 %collective-permute-start.3 = (f32[328,128]{1,0:T(8,128)S(1)}, f32[328,128]{1,0:T(8,128)S(1)}, u32[]{:S(2)}, u32[]{:S(2)}) collective-permute-start(f32[328,128]{1,0:T(8,128)S(1)} %get-tuple-element.23.refs_1_.refs_10_), channel_id=1, source_target_pairs={{1,2},{2,1},{3,4},{4,3},{5,6},{6,5},{7,8},{8,7},{9,10},{10,9},{11,... | collective-permute-start | bytes 503816 | tf_op jit(solution)/shard_map/ppermute | solution.py:418
  44.2 1.9 %collective-permute-start.2 = (f32[328,128]{1,0:T(8,128)S(1)}, f32[328,128]{1,0:T(8,128)S(1)}, u32[]{:S(2)}, u32[]{:S(2)}) collective-permute-start(f32[328,128]{1,0:T(8,128)S(1)} %get-tuple-element.23.refs_1_.refs_10_), channel_id=1, source_target_pairs={{0,1},{1,0},{2,3},{3,2},{4,5},{5,4},{6,7},{7,6},{8,9},{9,8},{10,11... | collective-permute-start | bytes 503816 | tf_op jit(solution)/shard_map/ppermute | solution.py:417
  46.2 3.2 %collective-permute-start.4 = (f32[8,128]{1,0:T(8,128)S(1)}, f32[8,128]{1,0:T(8,128)S(1)}, u32[]{:S(2)}, u32[]{:S(2)}) collective-permute-start(f32[8,128]{1,0:T(8,128)S(1)} %add.58.speed_ref.refs_9_), channel_id=1, source_target_pairs={{0,4},{1,5},{2,6},{3,7},{4,0},{5,1},{6,2},{7,3},{8,12},{9,13},{10,... | collective-permute-start | bytes 12296 | tf_op jit(solution)/shard_map/ppermute | solution.py:394
  49.4 1.1 %collective-permute-done.4.refs_10_ = f32[8,128]{1,0:T(8,128)S(1)} collective-permute-done((f32[8,128]{1,0:T(8,128)S(1)}, f32[8,128]{1,0:T(8,128)S(1)}, u32[]{:S(2)}, u32[]{:S(2)}) %collective-permute-start.4) | collective-permute-done | bytes 4128 | tf_op jit(solution)/shard_map/ppermute | solution.py:394
  50.5 0.0 collective-permute-done.3.refs_3_
  50.5 0.0 collective-permute-done.2.refs_2_
  50.5 0.7 shard_map.77
  51.2 4.4 %collective-permute-start.7 = (f32[328,128]{1,0:T(8,128)S(1)}, f32[328,128]{1,0:T(8,128)S(1)}, u32[]{:S(2)}, u32[]{:S(2)}) collective-permute-start(f32[328,128]{1,0:T(8,128)S(1)} %get-tuple-element.29.refs_11_), channel_id=1, source_target_pairs={{1,2},{2,1},{3,4},{4,3},{5,6},{6,5},{7,8},{8,7},{9,10},{10,9},{11,... | collective-permute-start | bytes 503816 | tf_op jit(solution)/shard_map/ppermute | solution.py:418
  55.6 1.9 %collective-permute-start.6 = (f32[328,128]{1,0:T(8,128)S(1)}, f32[328,128]{1,0:T(8,128)S(1)}, u32[]{:S(2)}, u32[]{:S(2)}) collective-permute-start(f32[328,128]{1,0:T(8,128)S(1)} %get-tuple-element.29.refs_11_), channel_id=1, source_target_pairs={{0,1},{1,0},{2,3},{3,2},{4,5},{5,4},{6,7},{7,6},{8,9},{9,8},{10,11... | collective-permute-start | bytes 503816 | tf_op jit(solution)/shard_map/ppermute | solution.py:417
  57.5 4.5 %collective-permute-start.5 = (f32[8,128]{1,0:T(8,128)S(1)}, f32[8,128]{1,0:T(8,128)S(1)}, u32[]{:S(2)}, u32[]{:S(2)}) collective-permute-start(f32[8,128]{1,0:T(8,128)S(1)} %get-tuple-element.28.refs_9_), channel_id=1, source_target_pairs={{0,8},{1,9},{2,10},{3,11},{4,12},{5,13},{6,14},{7,15},{8,0},{9,1},... | collective-permute-start | bytes 12296 | tf_op jit(solution)/shard_map/ppermute | solution.py:394
  62.1 1.3 %collective-permute-done.5.refs_10_ = f32[8,128]{1,0:T(8,128)S(1)} collective-permute-done((f32[8,128]{1,0:T(8,128)S(1)}, f32[8,128]{1,0:T(8,128)S(1)}, u32[]{:S(2)}, u32[]{:S(2)}) %collective-permute-start.5) | collective-permute-done | bytes 4128 | tf_op jit(solution)/shard_map/ppermute | solution.py:394
  63.4 0.0 collective-permute-done.7.refs_13_
  63.4 0.0 collective-permute-done.6.refs_12_
  63.4 0.7 shard_map.78
  64.2 5.0 %collective-permute-start.9 = (f32[328,128]{1,0:T(8,128)S(1)}, f32[328,128]{1,0:T(8,128)S(1)}, u32[]{:S(2)}, u32[]{:S(2)}) collective-permute-start(f32[328,128]{1,0:T(8,128)S(1)} %get-tuple-element.31.refs_1_), channel_id=1, source_target_pairs={{1,2},{2,1},{3,4},{4,3},{5,6},{6,5},{7,8},{8,7},{9,10},{10,9},{11,... | collective-permute-start | bytes 503816 | tf_op jit(solution)/shard_map/ppermute | solution.py:418
  69.2 1.9 %collective-permute-start.8 = (f32[328,128]{1,0:T(8,128)S(1)}, f32[328,128]{1,0:T(8,128)S(1)}, u32[]{:S(2)}, u32[]{:S(2)}) collective-permute-start(f32[328,128]{1,0:T(8,128)S(1)} %get-tuple-element.31.refs_1_), channel_id=1, source_target_pairs={{0,1},{1,0},{2,3},{3,2},{4,5},{5,4},{6,7},{7,6},{8,9},{9,8},{10,11... | collective-permute-start | bytes 503816 | tf_op jit(solution)/shard_map/ppermute | solution.py:417
  71.1 2.3 %collective-permute-done.9.refs_3_ = f32[328,128]{1,0:T(8,128)S(1)} collective-permute-done((f32[328,128]{1,0:T(8,128)S(1)}, f32[328,128]{1,0:T(8,128)S(1)}, u32[]{:S(2)}, u32[]{:S(2)}) %collective-permute-start.9) | collective-permute-done | bytes 167968 | tf_op jit(solution)/shard_map/ppermute | solution.py:418
  73.4 0.0 collective-permute-done.8.refs_2_
  73.4 0.7 shard_map.79
  74.1 3.9 %collective-permute-start.11 = (f32[328,128]{1,0:T(8,128)S(1)}, f32[328,128]{1,0:T(8,128)S(1)}, u32[]{:S(2)}, u32[]{:S(2)}) collective-permute-start(f32[328,128]{1,0:T(8,128)S(1)} %get-tuple-element.34.refs_1_), channel_id=1, source_target_pairs={{1,2},{2,1},{3,4},{4,3},{5,6},{6,5},{7,8},{8,7},{9,10},{10,9},{11,... | collective-permute-start | bytes 503816 | tf_op jit(solution)/shard_map/ppermute | solution.py:418
  78.0 1.9 %collective-permute-start.10 = (f32[328,128]{1,0:T(8,128)S(1)}, f32[328,128]{1,0:T(8,128)S(1)}, u32[]{:S(2)}, u32[]{:S(2)}) collective-permute-start(f32[328,128]{1,0:T(8,128)S(1)} %get-tuple-element.34.refs_1_), channel_id=1, source_target_pairs={{0,1},{1,0},{2,3},{3,2},{4,5},{5,4},{6,7},{7,6},{8,9},{9,8},{10,11... | collective-permute-start | bytes 503816 | tf_op jit(solution)/shard_map/ppermute | solution.py:417
  80.0 3.3 %collective-permute-done.11.refs_3_ = f32[328,128]{1,0:T(8,128)S(1)} collective-permute-done((f32[328,128]{1,0:T(8,128)S(1)}, f32[328,128]{1,0:T(8,128)S(1)}, u32[]{:S(2)}, u32[]{:S(2)}) %collective-permute-start.11) | collective-permute-done | bytes 167968 | tf_op jit(solution)/shard_map/ppermute | solution.py:418
  83.2 0.0 collective-permute-done.10.refs_2_
  83.2 1.0 shard_map.80
  84.2 25.8 %all_to_all.10.arrived_ref = f32[32,4,512]{2,1,0:T(4,128)S(1)} all-to-all(f32[32,4,512]{2,1,0:T(4,128)S(1)} %shard_map.80), channel_id=1, replica_groups=mesh['harm'=32,'slab'=16] {'harm'}, dimensions={0} | all-to-all | bytes 524288 | tf_op jit(solution)/shard_map/all_to_all | solution.py:448
  110.1 0.9 restore.1
  (3 shorter events, 0.0 us)
Async XLA Ops:
  3.1 34.7 %all-to-all-start = ((f32[32,4,384]{2,1,0:T(4,128)}), f32[32,4,384]{2,1,0:T(4,128)S(1)}, u32[]{:S(2)}, u32[]{:S(2)}) async-start(f32[32,4,384]{2,1,0:T(4,128)} %get-tuple-element.19), calls=%async_computation | async-start | bytes 393216 | tf_op jit(solution)/shard_map/all_to_all | solution.py:373
  21.9 4.0 %collective-permute-start = (f32[8,128]{1,0:T(8,128)S(1)}, f32[8,128]{1,0:T(8,128)S(1)}, u32[]{:S(2)}, u32[]{:S(2)}) collective-permute-start(f32[8,128]{1,0:T(8,128)S(1)} %get-tuple-element.22), channel_id=1, source_target_pairs={{0,1},{1,0},{2,3},{3,2},{4,5},{5,4},{6,7},{7,6},{8,9},{9,8},{10,11... | collective-permute-start | bytes 12296 | tf_op jit(solution)/shard_map/ppermute | solution.py:394
  25.8 4.6 %collective-permute-start.1 = (f32[8,128]{1,0:T(8,128)S(1)}, f32[8,128]{1,0:T(8,128)S(1)}, u32[]{:S(2)}, u32[]{:S(2)}) collective-permute-start(f32[8,128]{1,0:T(8,128)S(1)} %add.57), channel_id=1, source_target_pairs={{0,2},{1,3},{2,0},{3,1},{4,6},{5,7},{6,4},{7,5},{8,10},{9,11},{10,... | collective-permute-start | bytes 12296 | tf_op jit(solution)/shard_map/ppermute | solution.py:394
  37.9 12.6 %collective-permute-start.3 = (f32[328,128]{1,0:T(8,128)S(1)}, f32[328,128]{1,0:T(8,128)S(1)}, u32[]{:S(2)}, u32[]{:S(2)}) collective-permute-start(f32[328,128]{1,0:T(8,128)S(1)} %get-tuple-element.23.refs_1_.refs_10_), channel_id=1, source_target_pairs={{1,2},{2,1},{3,4},{4,3},{5,6},{6,5},{7,8},{8,7},{9,10},{10,9},{11,... | collective-permute-start | bytes 503816 | tf_op jit(solution)/shard_map/ppermute | solution.py:418
  44.2 6.3 %collective-permute-start.2 = (f32[328,128]{1,0:T(8,128)S(1)}, f32[328,128]{1,0:T(8,128)S(1)}, u32[]{:S(2)}, u32[]{:S(2)}) collective-permute-start(f32[328,128]{1,0:T(8,128)S(1)} %get-tuple-element.23.refs_1_.refs_10_), channel_id=1, source_target_pairs={{0,1},{1,0},{2,3},{3,2},{4,5},{5,4},{6,7},{7,6},{8,9},{9,8},{10,11... | collective-permute-start | bytes 503816 | tf_op jit(solution)/shard_map/ppermute | solution.py:417
  46.2 4.4 %collective-permute-start.4 = (f32[8,128]{1,0:T(8,128)S(1)}, f32[8,128]{1,0:T(8,128)S(1)}, u32[]{:S(2)}, u32[]{:S(2)}) collective-permute-start(f32[8,128]{1,0:T(8,128)S(1)} %add.58.speed_ref.refs_9_), channel_id=1, source_target_pairs={{0,4},{1,5},{2,6},{3,7},{4,0},{5,1},{6,2},{7,3},{8,12},{9,13},{10,... | collective-permute-start | bytes 12296 | tf_op jit(solution)/shard_map/ppermute | solution.py:394
  51.2 12.2 %collective-permute-start.7 = (f32[328,128]{1,0:T(8,128)S(1)}, f32[328,128]{1,0:T(8,128)S(1)}, u32[]{:S(2)}, u32[]{:S(2)}) collective-permute-start(f32[328,128]{1,0:T(8,128)S(1)} %get-tuple-element.29.refs_11_), channel_id=1, source_target_pairs={{1,2},{2,1},{3,4},{4,3},{5,6},{6,5},{7,8},{8,7},{9,10},{10,9},{11,... | collective-permute-start | bytes 503816 | tf_op jit(solution)/shard_map/ppermute | solution.py:418
  55.6 7.8 %collective-permute-start.6 = (f32[328,128]{1,0:T(8,128)S(1)}, f32[328,128]{1,0:T(8,128)S(1)}, u32[]{:S(2)}, u32[]{:S(2)}) collective-permute-start(f32[328,128]{1,0:T(8,128)S(1)} %get-tuple-element.29.refs_11_), channel_id=1, source_target_pairs={{0,1},{1,0},{2,3},{3,2},{4,5},{5,4},{6,7},{7,6},{8,9},{9,8},{10,11... | collective-permute-start | bytes 503816 | tf_op jit(solution)/shard_map/ppermute | solution.py:417
  57.5 5.9 %collective-permute-start.5 = (f32[8,128]{1,0:T(8,128)S(1)}, f32[8,128]{1,0:T(8,128)S(1)}, u32[]{:S(2)}, u32[]{:S(2)}) collective-permute-start(f32[8,128]{1,0:T(8,128)S(1)} %get-tuple-element.28.refs_9_), channel_id=1, source_target_pairs={{0,8},{1,9},{2,10},{3,11},{4,12},{5,13},{6,14},{7,15},{8,0},{9,1},... | collective-permute-start | bytes 12296 | tf_op jit(solution)/shard_map/ppermute | solution.py:394
  64.2 9.2 %collective-permute-start.9 = (f32[328,128]{1,0:T(8,128)S(1)}, f32[328,128]{1,0:T(8,128)S(1)}, u32[]{:S(2)}, u32[]{:S(2)}) collective-permute-start(f32[328,128]{1,0:T(8,128)S(1)} %get-tuple-element.31.refs_1_), channel_id=1, source_target_pairs={{1,2},{2,1},{3,4},{4,3},{5,6},{6,5},{7,8},{8,7},{9,10},{10,9},{11,... | collective-permute-start | bytes 503816 | tf_op jit(solution)/shard_map/ppermute | solution.py:418
  69.2 4.2 %collective-permute-start.8 = (f32[328,128]{1,0:T(8,128)S(1)}, f32[328,128]{1,0:T(8,128)S(1)}, u32[]{:S(2)}, u32[]{:S(2)}) collective-permute-start(f32[328,128]{1,0:T(8,128)S(1)} %get-tuple-element.31.refs_1_), channel_id=1, source_target_pairs={{0,1},{1,0},{2,3},{3,2},{4,5},{5,4},{6,7},{7,6},{8,9},{9,8},{10,11... | collective-permute-start | bytes 503816 | tf_op jit(solution)/shard_map/ppermute | solution.py:417
  74.1 9.1 %collective-permute-start.11 = (f32[328,128]{1,0:T(8,128)S(1)}, f32[328,128]{1,0:T(8,128)S(1)}, u32[]{:S(2)}, u32[]{:S(2)}) collective-permute-start(f32[328,128]{1,0:T(8,128)S(1)} %get-tuple-element.34.refs_1_), channel_id=1, source_target_pairs={{1,2},{2,1},{3,4},{4,3},{5,6},{6,5},{7,8},{8,7},{9,10},{10,9},{11,... | collective-permute-start | bytes 503816 | tf_op jit(solution)/shard_map/ppermute | solution.py:418
  78.0 5.2 %collective-permute-start.10 = (f32[328,128]{1,0:T(8,128)S(1)}, f32[328,128]{1,0:T(8,128)S(1)}, u32[]{:S(2)}, u32[]{:S(2)}) collective-permute-start(f32[328,128]{1,0:T(8,128)S(1)} %get-tuple-element.34.refs_1_), channel_id=1, source_target_pairs={{0,1},{1,0},{2,3},{3,2},{4,5},{5,4},{6,7},{7,6},{8,9},{9,8},{10,11... | collective-permute-start | bytes 503816 | tf_op jit(solution)/shard_map/ppermute | solution.py:417
